TPU v7x, 32 devices: a whole 2x2x4 slice. The times are simulated.
32 devices in a mesh: row: 4 (over y, core), col: 8 (over z, x).
Axes of the slice: x: 2, y: 2, z: 4, core: 2. Of those that a mesh axis runs over, the one named last changes fastest.
Arguments:
- eigvecs: float32 [1024, 50176], P('col', 'row'), may hold values from -6 to 6
- span_vectors: float32 [2, 32, 4, 128], P(None, 'row'), may hold values from -6 to 6
- span_offsets: int32 [2, 32], P(None, 'row'), may hold values from 0 to 12543, as said below
- panels: bfloat16 [2, 256, 50176], P(None, 'col', 'row'), may hold values from -0.026785714 to 0.026785714
Outputs:
- back_vectors: float32 [1024, 50176], P('col', 'row')
Inputs may be any that keep to these rules, and one draw needn't show every extreme that they name: `span_offsets`: each block starts within the rows of its index of row and ends at most 128 rows after them, and inside the matrix; on every index of row but the last the last block of each sweep reaches into the next index's rows.
All inputs are finite; a program needn't handle non-finite values.
Results may differ from a plain program's by a relative error of at most 0.0075.
Values may be sent and summed in bfloat16 or wider, within the bound.
A program may use at most 128 MiB of HBM per device.

v0:
```python
import functools

import jax
import jax.numpy as jnp
from jax import lax
from jax.experimental import pallas as pl
from jax.experimental.pallas import tpu as pltpu
from jax.sharding import PartitionSpec as P

PRECISE = lax.Precision.HIGHEST
LAST = (((1,), (1,)), ((), ()))
INNER = (((1,), (0,)), ((), ()))
LANES = 128
F32 = jnp.float32
BF16 = jnp.bfloat16
UP, DOWN, ACROSS = 0, 1, 2


def tile_of(rows_dev, most):
    count = rows_dev // LANES
    return LANES * max(part for part in range(1, most + 1) if count % part == 0)


def halves(value):
    high = value.astype(BF16)
    return high, (value - high.astype(F32)).astype(BF16)


def dot_split(left, right, dims):
    (left_high, left_low), (right_high, right_low) = left, right
    dot = functools.partial(lax.dot_general, dimension_numbers=dims, preferred_element_type=F32)
    return dot(left_high, right_high) + (dot(left_high, right_low) + dot(left_low, right_high))


def precise_dot(left, right, dims=INNER):
    return lax.dot_general(left, right, dims, precision=PRECISE, preferred_element_type=F32)


def triangle_inverse(matrix, down_at, across_at):
    order = matrix.shape[0]
    same = down_at == across_at
    diagonal = jnp.where(same, matrix, 0.0)
    down = 1.0 / jnp.sum(diagonal, axis=1, keepdims=True)
    across = 1.0 / jnp.sum(diagonal, axis=0, keepdims=True)
    inverse = jnp.where(same, down, 0.0)
    beside = (down_at // 2 == across_at // 2) & (down_at != across_at)
    inverse = inverse - jnp.where(beside, matrix * down * across, 0.0)
    size = 2
    while size < order:
        together = down_at // (2 * size) == across_at // (2 * size)
        beside = together & (down_at // size != across_at // size)
        off = jnp.where(beside, matrix, 0.0)
        inverse = inverse - precise_dot(inverse, precise_dot(off, inverse))
        size *= 2
    return inverse


def kernel(
    eig_ref, vec_ref, off_ref, pan_ref, out_ref,
    eig, wall, low, high, base, tail_out, tail_in, pack, sums, got,
    load_sem, own_sem, recv_sem, send_sem, tail_sem, pack_send, pack_recv, sum_send, sum_recv, out_sem,
):
    rows, cols = lax.axis_size("row"), lax.axis_size("col")
    line = cols // 2
    row, col = lax.axis_index("row"), lax.axis_index("col")
    at, side = col // 2, col % 2
    columns, rows_dev = eig.shape
    panels, _, width_own, _ = wall.shape
    width = cols * width_own
    sweeps, spans, refl, band = vec_ref.shape
    own = sweeps * spans * refl
    total = rows * own
    chunk = tile_of(rows_dev, 14)
    chunks = rows_dev // chunk
    tiles = rows_dev // LANES
    group = tile_of(rows_dev, 7)
    groups = rows_dev // group
    last = panels - 1
    beside = at + 1 - 2 * (at % 2)

    def cut(index):
        return pl.ds(pl.multiple_of(index * chunk, chunk), chunk)

    def target(way):
        if way == ACROSS:
            return {"col": col + 1 - 2 * side}
        return {"col": col + 2 if way == UP else col - 2}

    def copy(way, panel, origin, index, mine=False):
        where = wall.at[panel, origin, :, cut(index)]
        return pltpu.make_async_remote_copy(
            src_ref=pan_ref.at[panel, :, cut(index)] if mine else where,
            dst_ref=where,
            send_sem=send_sem.at[way, panel, origin],
            recv_sem=recv_sem.at[panel, origin, index],
            device_id=target(way),
            device_id_type=pl.DeviceIdType.MESH,
        )

    def send(way, panel, origin, index, mine=False):
        def start():
            copy(way, panel, origin, index, mine).start()

        if way == UP:
            pl.when(at < line - 1)(start)
        elif way == DOWN:
            pl.when(at > 0)(start)
        else:
            start()

    def send_own(way, panel):
        @pl.loop(0, chunks)
        def _(index):
            send(way, panel, col, index, True)

    def arrived(panel, origin, index):
        copy(ACROSS, panel, origin, index).wait_recv()

    def goes_across(panel, origin_at):
        return (origin_at != beside) if panel == last else (origin_at >= 0)

    def serve(panel, step, index):
        for way, source in ((UP, at - step), (DOWN, at + step)):
            @pl.when((source >= 0) & (source < line))
            def _(way=way, source=source):
                origin = 2 * source + side
                arrived(panel, origin, index)
                send(way, panel, origin, index)

                @pl.when(goes_across(panel, source))
                def _():
                    send(ACROSS, panel, origin, index)

    def serve_all(panel, step):
        @pl.loop(0, chunks)
        def _(index):
            serve(panel, step, index)

        if panel < last:
            @pl.when(at == step)
            def _():
                send_own(UP, panel + 1)

            @pl.when(at == line - 1 - step)
            def _():
                send_own(DOWN, panel + 1)

    def serve_partner(index):
        origin = 2 * at + 1 - side
        arrived(last, origin, index)

        @pl.when(at % 2 == 0)
        def _():
            send(UP, last, origin, index)

        @pl.when(at % 2 == 1)
        def _():
            send(DOWN, last, origin, index)

    def from_partner(panel, index):
        for source in range(line):
            def take(source=source):
                arrived(panel, 2 * source + 1 - side, index)

            if panel == last:
                pl.when(at != source)(take)
            else:
                take()

    barrier = pltpu.get_barrier_semaphore()

    def greet(where):
        pl.semaphore_signal(barrier, inc=1, device_id=where, device_id_type=pl.DeviceIdType.MESH)

    greet(target(ACROSS))
    pl.when(at > 0)(lambda: greet(target(DOWN)))
    pl.when(at < line - 1)(lambda: greet(target(UP)))
    for step in range(1, rows):
        greet({"row": lax.rem(row + step, rows)})
    neighbours = jnp.minimum(at, 1) + jnp.minimum(line - 1 - at, 1)
    pl.semaphore_wait(barrier, rows + neighbours)

    send_own(UP, 0)
    send_own(DOWN, 0)
    send_own(ACROSS, 0)
    load = pltpu.make_async_copy(eig_ref, eig, load_sem)
    load.start()
    for panel in range(panels):
        pltpu.make_async_copy(pan_ref.at[panel], wall.at[panel, col], own_sem.at[panel]).start()
    pl.when(at == 0)(lambda: send_own(UP, 1))
    pl.when(at == line - 1)(lambda: send_own(DOWN, 1))

    for index in range(sweeps * spans):
        low[index * refl : (index + 1) * refl, :] = vec_ref[index // spans, index % spans]
    per = 8 // refl
    for index in range(own // 8):
        rows_at = slice(8 * index, 8 * index + 8)
        spread = jnp.concatenate([low[rows_at, :], jnp.zeros((8, LANES), F32)], axis=1)
        moved = jnp.zeros_like(spread)
        first = jnp.zeros((8, LANES), jnp.int32)
        for part in range(per):
            span_at = index * per + part
            begin = off_ref[span_at // spans, span_at % spans]
            tile = begin // LANES
            turned = pltpu.roll(spread, begin - tile * LANES, 1)
            place = lax.broadcasted_iota(jnp.int32, (8, 2 * LANES), 0) // refl
            moved = jnp.where(place == part, turned, moved)
            first = jnp.where(place[:, :LANES] == part, tile, first)
        low[rows_at, :] = moved[:, :LANES]
        high[rows_at, :] = moved[:, LANES:]
        base[rows_at, :] = first

    def spans_at(tile):
        part = jnp.where(base[...] == tile, low[...], 0.0)
        return part + jnp.where(base[...] == tile - 1, high[...], 0.0)

    def spans_group(index):
        first = index * (group // LANES)
        return jnp.concatenate([spans_at(first + step) for step in range(group // LANES)], axis=1)

    def cut_group(index):
        return pl.ds(pl.multiple_of(index * group, group), group)

    tail_out[...] = jnp.where(base[...] == tiles - 1, high[...], 0.0)

    def tail_copy():
        return pltpu.make_async_remote_copy(
            src_ref=tail_out, dst_ref=tail_in, send_sem=tail_sem.at[0], recv_sem=tail_sem.at[1],
            device_id={"row": row + 1}, device_id_type=pl.DeviceIdType.MESH,
        )

    pl.when(row < rows - 1)(lambda: tail_copy().start())
    load.wait()

    def products(index, acc):
        spread = spans_group(index)
        left = jnp.concatenate([eig[:, cut_group(index)], spread], axis=0)
        right = jnp.concatenate([jnp.zeros_like(spread), spread], axis=0)
        return acc + dot_split(halves(left), halves(right), LAST)

    acc = lax.fori_loop(0, groups, products, jnp.zeros((columns + own, 2 * own), F32))
    pl.when(row > 0)(lambda: tail_copy().wait_recv())

    @pl.when(row == 0)
    def _():
        tail_in[...] = jnp.zeros_like(tail_in)

    before = tail_in[...]
    head = spans_at(0)
    nothing = jnp.zeros_like(before)
    left = jnp.concatenate([eig[:, :LANES], head], axis=0)
    acc = acc + dot_split(halves(left), halves(jnp.concatenate([before, nothing], axis=0)), LAST)
    tail = tail_out[...]
    beyond = dot_split(halves(tail), halves(jnp.concatenate([nothing, tail], axis=0)), LAST)
    pack[row, :columns, :] = acc[:columns]
    pack[row, columns : columns + own, :] = acc[columns:] + beyond
    pack[row, columns + own :, :] = dot_split(
        halves(before), halves(jnp.concatenate([head, nothing], axis=0)), LAST
    )

    def pack_copy(step):
        return pltpu.make_async_remote_copy(
            src_ref=pack.at[row], dst_ref=pack.at[row], send_sem=pack_send.at[step], recv_sem=pack_recv.at[row],
            device_id={"row": lax.rem(row + step, rows)}, device_id_type=pl.DeviceIdType.MESH,
        )

    def pack_taken(step):
        source = lax.rem(row + step, rows)
        return pltpu.make_async_remote_copy(
            src_ref=pack.at[source], dst_ref=pack.at[source], send_sem=pack_send.at[step], recv_sem=pack_recv.at[source],
            device_id={"row": source}, device_id_type=pl.DeviceIdType.MESH,
        )

    for step in range(1, rows):
        pack_copy(step).start()
    serve_all(0, 1) if line > 1 else None
    for step in range(1, rows):
        pack_taken(step).wait_recv()

    def placed(value, shift):
        wide = value
        if total > 2 * own:
            zeros = jnp.zeros((value.shape[0], total - 2 * own), F32)
            wide = jnp.concatenate([value, zeros], axis=1)
        shift = shift * own % total
        return pltpu.roll(wide, shift, 1) if shift else wide

    inner = jnp.zeros((columns, total), F32)
    blocks = []
    for index in range(rows):
        inner = inner + placed(pack[index, :columns, :], index - 1)
        block = placed(pack[index, columns : columns + own, :], index - 1)
        if index < rows - 1:
            block = block + placed(pack[index + 1, columns + own :, :], index + 1)
        blocks.append(block)
    matrix = jnp.concatenate(blocks, axis=0)
    orders = []
    for axis in range(2):
        value = lax.broadcasted_iota(jnp.int32, (total, total), axis)
        part, within = value // own, value % own
        sweep_own = spans * refl
        orders.append((within // sweep_own) * (rows * sweep_own) + part * sweep_own + within % sweep_own)
    down, over = orders
    earlier = (down // refl > over // refl) | ((down // refl == over // refl) & (down < over))
    matrix = jnp.where(earlier, matrix, jnp.where(down == over, 0.5 * matrix, 0.0))
    coeffs = precise_dot(inner, triangle_inverse(matrix, down, over), LAST)
    coeffs = pltpu.roll(coeffs, lax.rem(total + own - own * row, total), 1)[:, : 2 * own]
    coeffs = halves(coeffs)
    for step in range(2, line - 1):
        serve_all(0, step)

    @pl.loop(0, groups)
    def _(index):
        spread = spans_group(index)
        right = jnp.concatenate([jnp.zeros_like(spread), spread], axis=0)
        eig[:, cut_group(index)] -= dot_split(coeffs, halves(right), INNER)

    eig[:, :LANES] -= dot_split(coeffs, halves(jnp.concatenate([before, nothing], axis=0)), INNER)
    if line > 2:
        serve_all(0, line - 1)
    for panel in range(1, panels):
        send_own(ACROSS, panel)

    for panel in range(panels):
        pltpu.make_async_copy(pan_ref.at[panel], wall.at[panel, col], own_sem.at[panel]).wait()

    def reflectors(panel, index):
        return jnp.concatenate([wall[panel, part, :, cut(index)] for part in range(cols)], axis=0)

    def add_sums(panel, index):
        reflect = reflectors(panel, index)
        left = jnp.concatenate([eig[:, cut(index)].astype(BF16), reflect], axis=0)
        sums[panel] += lax.dot_general(left, reflect, LAST, preferred_element_type=F32)

    def row_sum(panel):
        step, bit = 0, 1
        while bit < rows:
            low_bit = (row // bit) % 2
            move = pltpu.make_async_remote_copy(
                src_ref=sums.at[panel], dst_ref=got.at[panel, step],
                send_sem=sum_send.at[panel, step], recv_sem=sum_recv.at[panel, step],
                device_id={"row": row + bit * (1 - 2 * low_bit)}, device_id_type=pl.DeviceIdType.MESH,
            )
            move.start()
            move.wait()
            sums[panel] += got[panel, step]
            step, bit = step + 1, 2 * bit

    def solved(panel):
        down = lax.broadcasted_iota(jnp.int32, (width, width), 0)
        over = lax.broadcasted_iota(jnp.int32, (width, width), 1)
        gram = sums[panel, columns:, :]
        matrix = jnp.where(down < over, gram, jnp.where(down == over, 0.5 * gram, 0.0))
        inverse = triangle_inverse(matrix, down, over)
        return precise_dot(sums[panel, :columns, :], inverse, LAST).astype(BF16)

    def update(panel, index, coeffs):
        eig[:, cut(index)] -= lax.dot_general(coeffs, reflectors(panel, index), INNER, preferred_element_type=F32)

    for panel in range(panels):
        sums[panel] = jnp.zeros_like(sums[panel])

    @pl.loop(0, chunks)
    def _(index):
        from_partner(0, index)
        add_sums(0, index)
        if line > 1:
            serve(1, 1, index)

    row_sum(0)
    coeffs = solved(0)

    @pl.loop(0, chunks)
    def _(index):
        serve_partner(index)
        for step in range(2, line - 1):
            serve(1, step, index)
        update(0, index, coeffs)

    if line > 2:
        @pl.loop(0, chunks)
        def _(index):
            serve(1, line - 1, index)

    @pl.loop(0, chunks)
    def _(index):
        from_partner(1, index)
        add_sums(1, index)

    row_sum(1)
    coeffs = solved(1)

    def out_copy(index):
        return pltpu.make_async_copy(eig.at[:, cut(index)], out_ref.at[:, cut(index)], out_sem.at[index])

    @pl.loop(0, chunks)
    def _(index):
        update(1, index, coeffs)
        out_copy(index).start()

    def gone(way, panel, origin):
        def wait():
            piece = wall.at[panel, origin]
            pltpu.make_async_remote_copy(
                src_ref=piece, dst_ref=piece, send_sem=send_sem.at[way, panel, origin],
                recv_sem=recv_sem.at[panel, origin, 0], device_id=target(way),
                device_id_type=pl.DeviceIdType.MESH,
            ).wait_send()

        if way == UP:
            pl.when(at < line - 1)(wait)
        elif way == DOWN:
            pl.when(at > 0)(wait)
        else:
            wait()

    for panel in range(panels):
        for source in range(line):
            origin = 2 * source + side
            pl.when(at >= source)(lambda: gone(UP, panel, origin))
            pl.when(at <= source)(lambda: gone(DOWN, panel, origin))
            pl.when(goes_across(panel, jnp.int32(source)))(lambda: gone(ACROSS, panel, origin))
    pl.when(at % 2 == 0)(lambda: gone(UP, last, 2 * at + 1 - side))
    pl.when(at % 2 == 1)(lambda: gone(DOWN, last, 2 * at + 1 - side))
    pl.when(row < rows - 1)(lambda: tail_copy().wait_send())
    for step in range(1, rows):
        pack_copy(step).wait_send()

    @pl.loop(0, chunks)
    def _(index):
        out_copy(index).wait()


def local(eigvecs, span_vectors, span_offsets, panels):
    rows, cols = lax.axis_size("row"), lax.axis_size("col")
    columns, rows_dev = eigvecs.shape
    count, width_own, _ = panels.shape
    sweeps, spans, refl, band = span_vectors.shape
    own = sweeps * spans * refl
    width = width_own * cols
    steps = rows.bit_length() - 1
    chunks = rows_dev // tile_of(rows_dev, 14)
    vmem = pltpu.VMEM
    dma = pltpu.SemaphoreType.DMA
    return pl.pallas_call(
        kernel,
        out_shape=jax.ShapeDtypeStruct(eigvecs.shape, F32),
        in_specs=[
            pl.BlockSpec(memory_space=pl.ANY),
            pl.BlockSpec(memory_space=pltpu.VMEM),
            pl.BlockSpec(memory_space=pltpu.SMEM),
            pl.BlockSpec(memory_space=pl.ANY),
        ],
        out_specs=pl.BlockSpec(memory_space=pl.ANY),
        scratch_shapes=[
            vmem((columns, rows_dev), F32),
            vmem((count, cols, width_own, rows_dev), BF16),
            vmem((own, LANES), F32),
            vmem((own, LANES), F32),
            vmem((own, LANES), jnp.int32),
            vmem((own, LANES), F32),
            vmem((own, LANES), F32),
            vmem((rows, columns + 2 * own, 2 * own), F32),
            vmem((count, columns + width, width), F32),
            vmem((count, steps, columns + width, width), F32),
            dma,
            dma((count,)),
            dma((count, cols, chunks)),
            dma((3, count, cols)),
            dma((2,)),
            dma((rows,)),
            dma((rows,)),
            dma((count, steps)),
            dma((count, steps)),
            dma((chunks,)),
        ],
        compiler_params=pltpu.CompilerParams(
            collective_id=0, has_side_effects=True, vmem_limit_bytes=60 * 2**20
        ),
        cost_estimate=pl.CostEstimate(
            flops=8 * width * (width + columns) * rows_dev,
            bytes_accessed=8 * rows_dev * columns + 8 * width * rows_dev,
            transcendentals=0,
        ),
    )(eigvecs, span_vectors, span_offsets, panels)


def solution(mesh):
    return jax.shard_map(
        local,
        mesh=mesh,
        in_specs=(
            P("col", "row"),
            P(None, "row", None, None),
            P(None, "row"),
            P(None, "col", "row"),
        ),
        out_specs=P("col", "row"),
        check_vma=False,
    )
```

profile of v0, /device:TPU:0, one launch (start us, length us, event | category | flops | bytes accessed | tf_op | source)
XLA Modules:
  0.0 168.2 jit_solution(9491277824580410451)
XLA Ops:
  0.0 162.2 %shard_map.46 = f32[128,12544]{1,0:T(8,128)} custom-call(f32[128,12544]{1,0:T(8,128)} %eig_ref.1, f32[2,8,4,128]{3,2,1,0:T(4,128)} %vec_ref.1, s32[2,8]{1,0:T(2,128)} %off_ref.1, bf16[2,32,12544]{2,1,0:T(8,128)(2,1)} %pan_ref.1), custom_call_target="tpu_custom_call" | custom-call | flops 9865003008 | bytes 38535168 | tf_op jit(solution)/shard_map/pallas_call | solution.py:445
  162.2 6.0 %copy.6 = f32[128,12544]{1,0:T(8,128)} copy(f32[128,12544]{1,0:T(8,128)} %shard_map.46) | data formatting | bytes 12845056
where the time goes:
time: 168 us
  Pallas kernels  162 us (96%)
  local copies, waits for them, and re-layouts  5.98 us (4%)
    pallas_call x1, Pallas kernels, local(): pl.pallas_call(kernel, out_shape=jax.ShapeDtypeStruct(eigvecs.shape, F32)...  162 us
    unnamed x1, local copies, waits for them, and re-layouts  5.98 us

commit v1 on v0

--- a/solution.py
+++ b/solution.py
@@ -56,16 +56,17 @@
 
 
 def kernel(
-    eig_ref, vec_ref, off_ref, pan_ref, out_ref,
-    eig, wall, low, high, base, tail_out, tail_in, pack, sums, got,
-    load_sem, own_sem, recv_sem, send_sem, tail_sem, pack_send, pack_recv, sum_send, sum_recv, out_sem,
+    eig_ref, vec_ref, off_ref, pan_ref, eig, wall_last, coef_ref,
+    wall_first, low, high, base, tail_out, tail_in, pack, sums, got,
+    load_sem, own_sem, recv_sem, send_sem, tail_sem, pack_send, pack_recv, sum_send, sum_recv,
 ):
     rows, cols = lax.axis_size("row"), lax.axis_size("col")
     line = cols // 2
     row, col = lax.axis_index("row"), lax.axis_index("col")
     at, side = col // 2, col % 2
     columns, rows_dev = eig.shape
-    panels, _, width_own, _ = wall.shape
+    walls = (wall_first, wall_last)
+    panels, width_own, _ = pan_ref.shape
     width = cols * width_own
     sweeps, spans, refl, band = vec_ref.shape
     own = sweeps * spans * refl
@@ -87,7 +88,7 @@
         return {"col": col + 2 if way == UP else col - 2}
 
     def copy(way, panel, origin, index, mine=False):
-        where = wall.at[panel, origin, :, cut(index)]
+        where = walls[panel].at[origin, :, cut(index)]
         return pltpu.make_async_remote_copy(
             src_ref=pan_ref.at[panel, :, cut(index)] if mine else where,
             dst_ref=where,
@@ -186,7 +187,7 @@
     load = pltpu.make_async_copy(eig_ref, eig, load_sem)
     load.start()
     for panel in range(panels):
-        pltpu.make_async_copy(pan_ref.at[panel], wall.at[panel, col], own_sem.at[panel]).start()
+        pltpu.make_async_copy(pan_ref.at[panel], walls[panel].at[col], own_sem.at[panel]).start()
     pl.when(at == 0)(lambda: send_own(UP, 1))
     pl.when(at == line - 1)(lambda: send_own(DOWN, 1))
 
@@ -322,29 +323,34 @@
         send_own(ACROSS, panel)
 
     for panel in range(panels):
-        pltpu.make_async_copy(pan_ref.at[panel], wall.at[panel, col], own_sem.at[panel]).wait()
+        pltpu.make_async_copy(pan_ref.at[panel], walls[panel].at[col], own_sem.at[panel]).wait()
 
     def reflectors(panel, index):
-        return jnp.concatenate([wall[panel, part, :, cut(index)] for part in range(cols)], axis=0)
+        return jnp.concatenate([walls[panel][part, :, cut(index)] for part in range(cols)], axis=0)
 
     def add_sums(panel, index):
         reflect = reflectors(panel, index)
         left = jnp.concatenate([eig[:, cut(index)].astype(BF16), reflect], axis=0)
         sums[panel] += lax.dot_general(left, reflect, LAST, preferred_element_type=F32)
 
-    def row_sum(panel):
-        step, bit = 0, 1
-        while bit < rows:
-            low_bit = (row // bit) % 2
-            move = pltpu.make_async_remote_copy(
-                src_ref=sums.at[panel], dst_ref=got.at[panel, step],
-                send_sem=sum_send.at[panel, step], recv_sem=sum_recv.at[panel, step],
-                device_id={"row": row + bit * (1 - 2 * low_bit)}, device_id_type=pl.DeviceIdType.MESH,
-            )
-            move.start()
-            move.wait()
+    def row_move(panel, step):
+        bit = 2**step
+        low_bit = (row // bit) % 2
+        return pltpu.make_async_remote_copy(
+            src_ref=sums.at[panel], dst_ref=got.at[panel, step],
+            send_sem=sum_send.at[panel, step], recv_sem=sum_recv.at[panel, step],
+            device_id={"row": row + bit * (1 - 2 * low_bit)}, device_id_type=pl.DeviceIdType.MESH,
+        )
+
+    steps = rows.bit_length() - 1
+
+    def row_sum(panel, meanwhile=lambda: None):
+        for step in range(steps):
+            row_move(panel, step).start()
+            if step == steps - 1:
+                meanwhile()
+            row_move(panel, step).wait()
             sums[panel] += got[panel, step]
-            step, bit = step + 1, 2 * bit
 
     def solved(panel):
         down = lax.broadcasted_iota(jnp.int32, (width, width), 0)
@@ -367,14 +373,21 @@
         if line > 1:
             serve(1, 1, index)
 
-    row_sum(0)
+    def serve_between():
+        for step in range(2, line - 1):
+            @pl.loop(0, chunks)
+            def _(index):
+                serve(1, step, index)
+
+        @pl.loop(0, chunks)
+        def _(index):
+            serve_partner(index)
+
+    row_sum(0, serve_between)
     coeffs = solved(0)
 
     @pl.loop(0, chunks)
     def _(index):
-        serve_partner(index)
-        for step in range(2, line - 1):
-            serve(1, step, index)
         update(0, index, coeffs)
 
     if line > 2:
@@ -388,19 +401,11 @@
         add_sums(1, index)
 
     row_sum(1)
-    coeffs = solved(1)
-
-    def out_copy(index):
-        return pltpu.make_async_copy(eig.at[:, cut(index)], out_ref.at[:, cut(index)], out_sem.at[index])
-
-    @pl.loop(0, chunks)
-    def _(index):
-        update(1, index, coeffs)
-        out_copy(index).start()
+    coef_ref[...] = solved(1)
 
     def gone(way, panel, origin):
         def wait():
-            piece = wall.at[panel, origin]
+            piece = walls[panel].at[origin]
             pltpu.make_async_remote_copy(
                 src_ref=piece, dst_ref=piece, send_sem=send_sem.at[way, panel, origin],
                 recv_sem=recv_sem.at[panel, origin, 0], device_id=target(way),
@@ -426,9 +431,31 @@
     for step in range(1, rows):
         pack_copy(step).wait_send()
 
+
+def finish_kernel(eig_ref, wall_ref, coef_ref, out_ref, held, sems):
+    cols = wall_ref.shape[0]
+    rows_dev = eig_ref.shape[1]
+    chunk = tile_of(rows_dev, 14)
+    chunks = rows_dev // chunk
+
+    def cut(index):
+        return pl.ds(pl.multiple_of(index * chunk, chunk), chunk)
+
+    def copy(index):
+        return pltpu.make_async_copy(held.at[:, cut(index)], out_ref.at[:, cut(index)], sems.at[index])
+
+    coeffs = coef_ref[...]
+
     @pl.loop(0, chunks)
     def _(index):
-        out_copy(index).wait()
+        reflect = jnp.concatenate([wall_ref[part, :, cut(index)] for part in range(cols)], axis=0)
+        update = lax.dot_general(coeffs, reflect, INNER, preferred_element_type=F32)
+        held[:, cut(index)] = eig_ref[:, cut(index)] - update
+        copy(index).start()
+
+    @pl.loop(0, chunks)
+    def _(index):
+        copy(index).wait()
 
 
 def local(eigvecs, span_vectors, span_offsets, panels):
@@ -442,19 +469,22 @@
     chunks = rows_dev // tile_of(rows_dev, 14)
     vmem = pltpu.VMEM
     dma = pltpu.SemaphoreType.DMA
-    return pl.pallas_call(
+    eigen, wall, coeffs = pl.pallas_call(
         kernel,
-        out_shape=jax.ShapeDtypeStruct(eigvecs.shape, F32),
+        out_shape=(
+            vmem(eigvecs.shape, F32),
+            vmem((cols, width_own, rows_dev), BF16),
+            vmem((columns, width), BF16),
+        ),
         in_specs=[
-            pl.BlockSpec(memory_space=pl.ANY),
+            pl.BlockSpec(memory_space=pltpu.HBM),
             pl.BlockSpec(memory_space=pltpu.VMEM),
             pl.BlockSpec(memory_space=pltpu.SMEM),
-            pl.BlockSpec(memory_space=pl.ANY),
+            pl.BlockSpec(memory_space=pltpu.HBM),
         ],
-        out_specs=pl.BlockSpec(memory_space=pl.ANY),
+        out_specs=[pl.BlockSpec(memory_space=pltpu.VMEM)] * 3,
         scratch_shapes=[
-            vmem((columns, rows_dev), F32),
-            vmem((count, cols, width_own, rows_dev), BF16),
+            vmem((cols, width_own, rows_dev), BF16),
             vmem((own, LANES), F32),
             vmem((own, LANES), F32),
             vmem((own, LANES), jnp.int32),
@@ -472,10 +502,9 @@
             dma((rows,)),
             dma((count, steps)),
             dma((count, steps)),
-            dma((chunks,)),
         ],
         compiler_params=pltpu.CompilerParams(
-            collective_id=0, has_side_effects=True, vmem_limit_bytes=60 * 2**20
+            collective_id=0, has_side_effects=True, vmem_limit_bytes=40 * 2**20
         ),
         cost_estimate=pl.CostEstimate(
             flops=8 * width * (width + columns) * rows_dev,
@@ -483,6 +512,17 @@
             transcendentals=0,
         ),
     )(eigvecs, span_vectors, span_offsets, panels)
+    return pl.pallas_call(
+        finish_kernel,
+        out_shape=jax.ShapeDtypeStruct(eigvecs.shape, F32),
+        in_specs=[pl.BlockSpec(memory_space=pltpu.VMEM)] * 3,
+        out_specs=pl.BlockSpec(memory_space=pl.ANY),
+        scratch_shapes=[vmem(eigvecs.shape, F32), dma((chunks,))],
+        compiler_params=pltpu.CompilerParams(vmem_limit_bytes=16 * 2**20),
+        cost_estimate=pl.CostEstimate(
+            flops=2 * width * columns * rows_dev, bytes_accessed=8 * columns * rows_dev, transcendentals=0
+        ),
+    )(eigen, wall, coeffs)
 
 
 def solution(mesh):

time: 168 us -> 155 us (0.923)
  Pallas kernels: 162 us -> 152 us
  local copies, waits for them, and re-layouts: 5.98 us -> 2.85 us
    pallas_call x1 -> x2, Pallas kernels: 162 us -> 152 us  [the longest x1 149 us: local(): pl.pallas_call(kernel, out_shape=(vmem(eigvecs.shape, F32), vmem((cols, w...]
    unnamed x1 -> x6, local copies, waits for them, and re-layouts: 5.98 us -> 2.85 us
where the time goes in v1:
time: 155 us
  Pallas kernels  152 us (98%)
  local copies, waits for them, and re-layouts  2.85 us (2%)
    pallas_call x1, Pallas kernels, local(): pl.pallas_call(kernel, out_shape=(vmem(eigvecs.shape, F32), vmem((cols, w...  149 us

profile of v1, /device:TPU:0, one launch (start us, length us, event | category | flops | bytes accessed | tf_op | source)
XLA Modules:
  0.0 155.0 jit_solution(3937942063716787694)
XLA Ops:
  0.0 0.0 copy-start
  0.0 1.4 copy-done
  1.4 0.0 copy-start.1
  1.4 0.8 copy-done.1
  2.2 0.0 copy-start.2
  2.2 0.7 copy-done.2
  2.9 148.9 %shard_map.46 = (f32[128,12544]{1,0:T(8,128)S(1)}, bf16[8,32,12544]{2,1,0:T(8,128)(2,1)S(1)}, bf16[128,256]{1,0:T(8,128)(2,1)S(1)}) custom-call(f32[128,12544]{1,0:T(8,128)} %eig_ref.1, f32[2,8,4,128]{3,2,1,0:T(4,128)S(1)} %copy-done.1, s32[2,8]{1,0:T(2,128)S(1)} %copy-done.2, bf16[2,32,12544]{2,1,0:T(8,128)(2,1)S(1)} %copy-done), custom_call_target="tpu_custom_call" | custom-call | flops 9865003008 | bytes 38535168 | tf_op jit(solution)/shard_map/pallas_call | solution.py:472
  151.8 3.1 %shard_map.47 = f32[128,12544]{1,0:T(8,128)} custom-call(f32[128,12544]{1,0:T(8,128)S(1)} %get-tuple-element.8.eig_ref, bf16[8,32,12544]{2,1,0:T(8,128)(2,1)S(1)} %get-tuple-element.9.wall_ref, bf16[128,256]{1,0:T(8,128)(2,1)S(1)} %get-tuple-element.10.coef_ref), custom_call_target="tpu_custom_call" | custom-call | flops 822083584 | bytes 12845056 | tf_op jit(solution)/shard_map/pallas_call | solution.py:515
Async XLA Ops:
  0.0 1.4 copy-start
  1.4 0.8 copy-start.1
  2.2 0.7 copy-start.2

commit v2 on v1

--- a/solution.py
+++ b/solution.py
@@ -36,8 +36,7 @@
     return lax.dot_general(left, right, dims, precision=PRECISE, preferred_element_type=F32)
 
 
-def triangle_inverse(matrix, down_at, across_at):
-    order = matrix.shape[0]
+def triangle_inverse(matrix, down_at, across_at, order):
     same = down_at == across_at
     diagonal = jnp.where(same, matrix, 0.0)
     down = 1.0 / jnp.sum(diagonal, axis=1, keepdims=True)
@@ -55,10 +54,24 @@
     return inverse
 
 
+def last_order(cols, col):
+    line, at, side = cols // 2, col // 2, col % 2
+    beside = at + 1 - 2 * (at % 2)
+    far = (line - 1) * (1 - 2 * at // line)
+    first, second = jnp.minimum(beside, far), jnp.maximum(beside, far)
+    early = []
+    for index in range(line - 2):
+        place = index + jnp.where(first <= index, 1, 0)
+        early.append(place + jnp.where(second <= place, 1, 0))
+    order = [2 * place + side for place in range(line)]
+    return order + [2 * place + 1 - side for place in (*early, beside, far)]
+
+
 def kernel(
     eig_ref, vec_ref, off_ref, pan_ref, eig, wall_last, coef_ref,
-    wall_first, low, high, base, tail_out, tail_in, pack, sums, got,
+    wall_first, vecs, offs, low, high, base, tail_out, tail_in, pack, sums, got, late, late_got, corner, places,
     load_sem, own_sem, recv_sem, send_sem, tail_sem, pack_send, pack_recv, sum_send, sum_recv,
+    late_send, late_recv, corner_send, corner_recv,
 ):
     rows, cols = lax.axis_size("row"), lax.axis_size("col")
     line = cols // 2
@@ -68,7 +81,7 @@
     walls = (wall_first, wall_last)
     panels, width_own, _ = pan_ref.shape
     width = cols * width_own
-    sweeps, spans, refl, band = vec_ref.shape
+    sweeps, spans, refl, band = vecs.shape
     own = sweeps * spans * refl
     total = rows * own
     chunk = tile_of(rows_dev, 14)
@@ -78,6 +91,10 @@
     groups = rows_dev // group
     last = panels - 1
     beside = at + 1 - 2 * (at % 2)
+    order = last_order(cols, col)
+    late_width = 2 * width_own
+    early_width = width - late_width
+    fold = width_own // 8
 
     def cut(index):
         return pl.ds(pl.multiple_of(index * chunk, chunk), chunk)
@@ -158,15 +175,10 @@
         def _():
             send(DOWN, last, origin, index)
 
-    def from_partner(panel, index):
-        for source in range(line):
-            def take(source=source):
-                arrived(panel, 2 * source + 1 - side, index)
-
-            if panel == last:
-                pl.when(at != source)(take)
-            else:
-                take()
+    vec_load = pltpu.make_async_copy(vec_ref, vecs, load_sem.at[1])
+    off_load = pltpu.make_async_copy(off_ref, offs, load_sem.at[2])
+    vec_load.start()
+    off_load.start()
 
     barrier = pltpu.get_barrier_semaphore()
 
@@ -184,15 +196,18 @@
     send_own(UP, 0)
     send_own(DOWN, 0)
     send_own(ACROSS, 0)
-    load = pltpu.make_async_copy(eig_ref, eig, load_sem)
+    load = pltpu.make_async_copy(eig_ref, eig, load_sem.at[0])
     load.start()
     for panel in range(panels):
         pltpu.make_async_copy(pan_ref.at[panel], walls[panel].at[col], own_sem.at[panel]).start()
     pl.when(at == 0)(lambda: send_own(UP, 1))
     pl.when(at == line - 1)(lambda: send_own(DOWN, 1))
 
+    vec_load.wait()
+    off_load.wait()
+
     for index in range(sweeps * spans):
-        low[index * refl : (index + 1) * refl, :] = vec_ref[index // spans, index % spans]
+        low[index * refl : (index + 1) * refl, :] = vecs[index // spans, index % spans]
     per = 8 // refl
     for index in range(own // 8):
         rows_at = slice(8 * index, 8 * index + 8)
@@ -201,7 +216,7 @@
         first = jnp.zeros((8, LANES), jnp.int32)
         for part in range(per):
             span_at = index * per + part
-            begin = off_ref[span_at // spans, span_at % spans]
+            begin = offs[span_at // spans, span_at % spans]
             tile = begin // LANES
             turned = pltpu.roll(spread, begin - tile * LANES, 1)
             place = lax.broadcasted_iota(jnp.int32, (8, 2 * LANES), 0) // refl
@@ -231,6 +246,15 @@
         )
 
     pl.when(row < rows - 1)(lambda: tail_copy().start())
+    for panel in range(panels):
+        pltpu.make_async_copy(pan_ref.at[panel], walls[panel].at[col], own_sem.at[panel]).wait()
+
+    def own_products(index, acc):
+        mine = walls[last][col, :, cut(index)]
+        padded = jnp.concatenate([mine, jnp.zeros((LANES - width_own, chunk), BF16)], axis=0)
+        return acc + lax.dot_general(mine, padded, LAST, preferred_element_type=F32)
+
+    pack[row, columns + 2 * own :, :] = lax.fori_loop(0, chunks, own_products, jnp.zeros((width_own, LANES), F32))
     load.wait()
 
     def products(index, acc):
@@ -255,7 +279,7 @@
     beyond = dot_split(halves(tail), halves(jnp.concatenate([nothing, tail], axis=0)), LAST)
     pack[row, :columns, :] = acc[:columns]
     pack[row, columns : columns + own, :] = acc[columns:] + beyond
-    pack[row, columns + own :, :] = dot_split(
+    pack[row, columns + own : columns + 2 * own, :] = dot_split(
         halves(before), halves(jnp.concatenate([head, nothing], axis=0)), LAST
     )
 
@@ -277,6 +301,50 @@
     serve_all(0, 1) if line > 1 else None
     for step in range(1, rows):
         pack_taken(step).wait_recv()
+
+    square = pack[0, columns + 2 * own :, :]
+    for index in range(1, rows):
+        square = square + pack[index, columns + 2 * own :, :]
+    square = square[:, :width_own]
+    down = lax.broadcasted_iota(jnp.int32, (width_own, width_own), 0)
+    over = lax.broadcasted_iota(jnp.int32, (width_own, width_own), 1)
+    square = jnp.where(down < over, square, jnp.where(down == over, 0.5 * square, 0.0))
+    square = triangle_inverse(square, down, over, width_own)
+    square = jnp.concatenate([square, jnp.zeros((width_own, LANES - width_own), F32)], axis=1)
+    folded = square[:8]
+    for index in range(1, fold):
+        folded = folded + pltpu.roll(square[8 * index : 8 * index + 8], index * width_own, 1)
+    corner[col] = folded
+
+    def corner_copy(way, origin):
+        return pltpu.make_async_remote_copy(
+            src_ref=corner.at[origin], dst_ref=corner.at[origin],
+            send_sem=corner_send.at[way, origin], recv_sem=corner_recv.at[origin],
+            device_id=target(way), device_id_type=pl.DeviceIdType.MESH,
+        )
+
+    def send_corner(way, origin):
+        def start():
+            corner_copy(way, origin).start()
+
+        if way == UP:
+            pl.when(at < line - 1)(start)
+        elif way == DOWN:
+            pl.when(at > 0)(start)
+        else:
+            start()
+
+    def serve_corner(step):
+        for way, source in ((UP, at - step), (DOWN, at + step)):
+            @pl.when((source >= 0) & (source < line))
+            def _(way=way, source=source):
+                origin = 2 * source + side
+                corner_copy(way, origin).wait_recv()
+                send_corner(way, origin)
+                send_corner(ACROSS, origin)
+
+    for way in (UP, DOWN, ACROSS):
+        send_corner(way, col)
 
     def placed(value, shift):
         wide = value
@@ -292,7 +360,7 @@
         inner = inner + placed(pack[index, :columns, :], index - 1)
         block = placed(pack[index, columns : columns + own, :], index - 1)
         if index < rows - 1:
-            block = block + placed(pack[index + 1, columns + own :, :], index + 1)
+            block = block + placed(pack[index + 1, columns + own : columns + 2 * own, :], index + 1)
         blocks.append(block)
     matrix = jnp.concatenate(blocks, axis=0)
     orders = []
@@ -304,7 +372,7 @@
     down, over = orders
     earlier = (down // refl > over // refl) | ((down // refl == over // refl) & (down < over))
     matrix = jnp.where(earlier, matrix, jnp.where(down == over, 0.5 * matrix, 0.0))
-    coeffs = precise_dot(inner, triangle_inverse(matrix, down, over), LAST)
+    coeffs = precise_dot(inner, triangle_inverse(matrix, down, over, total), LAST)
     coeffs = pltpu.roll(coeffs, lax.rem(total + own - own * row, total), 1)[:, : 2 * own]
     coeffs = halves(coeffs)
     for step in range(2, line - 1):
@@ -319,59 +387,93 @@
     eig[:, :LANES] -= dot_split(coeffs, halves(jnp.concatenate([before, nothing], axis=0)), INNER)
     if line > 2:
         serve_all(0, line - 1)
+    serve_corner(1)
     for panel in range(1, panels):
         send_own(ACROSS, panel)
 
-    for panel in range(panels):
-        pltpu.make_async_copy(pan_ref.at[panel], walls[panel].at[col], own_sem.at[panel]).wait()
-
-    def reflectors(panel, index):
-        return jnp.concatenate([walls[panel][part, :, cut(index)] for part in range(cols)], axis=0)
-
-    def add_sums(panel, index):
-        reflect = reflectors(panel, index)
-        left = jnp.concatenate([eig[:, cut(index)].astype(BF16), reflect], axis=0)
-        sums[panel] += lax.dot_general(left, reflect, LAST, preferred_element_type=F32)
-
-    def row_move(panel, step):
+    def reflectors(panel, index, parts):
+        return jnp.concatenate([walls[panel][part, :, cut(index)] for part in parts], axis=0)
+
+    def rounded(index):
+        return eig[:, cut(index)].astype(BF16)
+
+    def row_copy(source, dest, send, recv, step):
         bit = 2**step
         low_bit = (row // bit) % 2
         return pltpu.make_async_remote_copy(
-            src_ref=sums.at[panel], dst_ref=got.at[panel, step],
-            send_sem=sum_send.at[panel, step], recv_sem=sum_recv.at[panel, step],
+            src_ref=source, dst_ref=dest, send_sem=send, recv_sem=recv,
             device_id={"row": row + bit * (1 - 2 * low_bit)}, device_id_type=pl.DeviceIdType.MESH,
         )
 
     steps = rows.bit_length() - 1
-
-    def row_sum(panel, meanwhile=lambda: None):
+    kept = (columns + width, columns + early_width)
+
+    def row_sum(panel, meanwhile):
+        rows_at = pl.ds(0, kept[panel])
         for step in range(steps):
-            row_move(panel, step).start()
+            move = row_copy(
+                sums.at[panel, rows_at], got.at[panel, step, rows_at],
+                sum_send.at[panel, step], sum_recv.at[panel, step], step,
+            )
+            move.start()
             if step == steps - 1:
                 meanwhile()
-            row_move(panel, step).wait()
-            sums[panel] += got[panel, step]
-
-    def solved(panel):
+            move.wait()
+            sums[panel, rows_at, :] += got[panel, step, rows_at, :]
+
+    def triangle(gram):
         down = lax.broadcasted_iota(jnp.int32, (width, width), 0)
         over = lax.broadcasted_iota(jnp.int32, (width, width), 1)
-        gram = sums[panel, columns:, :]
         matrix = jnp.where(down < over, gram, jnp.where(down == over, 0.5 * gram, 0.0))
-        inverse = triangle_inverse(matrix, down, over)
-        return precise_dot(sums[panel, :columns, :], inverse, LAST).astype(BF16)
-
-    def update(panel, index, coeffs):
-        eig[:, cut(index)] -= lax.dot_general(coeffs, reflectors(panel, index), INNER, preferred_element_type=F32)
+        return triangle_inverse(matrix, down, over, width)
+
+    def diagonal(parts):
+        stack = []
+        for part in parts:
+            folded = corner[part]
+            stack.append(folded)
+            for index in range(1, fold):
+                stack.append(pltpu.roll(folded, LANES - index * width_own, 1))
+        stack = jnp.concatenate(stack, axis=0)
+        down = lax.broadcasted_iota(jnp.int32, (LANES, width), 0)
+        over = lax.broadcasted_iota(jnp.int32, (LANES, width), 1) % width_own
+        wide = precise_dot(stack, jnp.where(down == over, 1.0, 0.0).astype(F32))
+        down = lax.broadcasted_iota(jnp.int32, (width, width), 0) // width_own
+        over = lax.broadcasted_iota(jnp.int32, (width, width), 1) // width_own
+        return jnp.where(down == over, wide, 0.0)
+
+    def set_places(parts):
+        for axis in range(2):
+            part_at = lax.broadcasted_iota(jnp.int32, (width, width), axis) // width_own
+            place = jnp.zeros_like(part_at)
+            for index, part in enumerate(parts):
+                place = jnp.where(part_at == index, part, place)
+            places[axis] = place
+
+    def solved(gram, inner, inverse):
+        size = 1
+        while size < cols:
+            down, over = places[0], places[1]
+            off = (down // (2 * size) == over // (2 * size)) & (down // size < over // size)
+            off = halves(jnp.where(off, gram, 0.0))
+            split = halves(inverse)
+            inverse = inverse - dot_split(split, halves(dot_split(off, split, INNER)), INNER)
+            size *= 2
+        return dot_split(halves(inner), halves(inverse), LAST).astype(BF16)
 
     for panel in range(panels):
         sums[panel] = jnp.zeros_like(sums[panel])
+    late[...] = jnp.zeros_like(late)
+    natural = list(range(cols))
 
     @pl.loop(0, chunks)
     def _(index):
-        from_partner(0, index)
-        add_sums(0, index)
-        if line > 1:
-            serve(1, 1, index)
+        for source in range(line):
+            arrived(0, 2 * source + 1 - side, index)
+        reflect = reflectors(0, index, natural)
+        left = jnp.concatenate([rounded(index), reflect], axis=0)
+        sums[0] += lax.dot_general(left, reflect, LAST, preferred_element_type=F32)
+        serve(1, 1, index)
 
     def serve_between():
         for step in range(2, line - 1):
@@ -383,26 +485,45 @@
         def _(index):
             serve_partner(index)
 
+    if line > 2:
+        serve_corner(2)
     row_sum(0, serve_between)
-    coeffs = solved(0)
+    for step in range(3, line):
+        serve_corner(step)
+    coeffs = precise_dot(sums[0, :columns, :], triangle(sums[0, columns:, :]), LAST).astype(BF16)
 
     @pl.loop(0, chunks)
     def _(index):
-        update(0, index, coeffs)
-
-    if line > 2:
-        @pl.loop(0, chunks)
-        def _(index):
-            serve(1, line - 1, index)
+        reflect = reflectors(0, index, natural)
+        eig[:, cut(index)] -= lax.dot_general(coeffs, reflect, INNER, preferred_element_type=F32)
+
+    early_parts, late_parts = order[:-2], order[-2:]
 
     @pl.loop(0, chunks)
     def _(index):
-        from_partner(1, index)
-        add_sums(1, index)
-
-    row_sum(1)
-    coef_ref[...] = solved(1)
-
+        serve(1, line - 1, index)
+        for source in range(line):
+            other = 2 * source + 1 - side
+            known = (at == source) | (late_parts[0] == other) | (late_parts[1] == other)
+            pl.when(jnp.logical_not(known))(lambda: arrived(1, other, index))
+        reflect = reflectors(1, index, early_parts)
+        left = jnp.concatenate([rounded(index), reflect], axis=0)
+        right = jnp.concatenate([reflect, jnp.zeros((late_width, chunk), BF16)], axis=0)
+        sums[1, pl.ds(0, kept[1]), :] += lax.dot_general(left, right, LAST, preferred_element_type=F32)
+
+    def add_late(index):
+        for part in late_parts:
+            arrived(1, part, index)
+        reflect = reflectors(1, index, late_parts)
+        right = jnp.concatenate([reflectors(1, index, order), rounded(index)], axis=0)
+        late[...] += lax.dot_general(reflect, right, LAST, preferred_element_type=F32)
+
+    for source in range(line):
+        corner_copy(ACROSS, 2 * source + 1 - side).wait_recv()
+    set_places(order)
+    row_sum(1, lambda: pl.loop(0, chunks - 1)(add_late))
+    inverse = diagonal(order)
+    add_late(chunks - 1)
     def gone(way, panel, origin):
         def wait():
             piece = walls[panel].at[origin]
@@ -419,17 +540,39 @@
         else:
             wait()
 
-    for panel in range(panels):
+    def all_gone():
+        for panel in range(panels):
+            for source in range(line):
+                origin = 2 * source + side
+                pl.when(at >= source)(lambda: gone(UP, panel, origin))
+                pl.when(at <= source)(lambda: gone(DOWN, panel, origin))
+                pl.when(goes_across(panel, jnp.int32(source)))(lambda: gone(ACROSS, panel, origin))
+        pl.when(at % 2 == 0)(lambda: gone(UP, last, 2 * at + 1 - side))
+        pl.when(at % 2 == 1)(lambda: gone(DOWN, last, 2 * at + 1 - side))
+        pl.when(row < rows - 1)(lambda: tail_copy().wait_send())
+        for step in range(1, rows):
+            pack_copy(step).wait_send()
         for source in range(line):
             origin = 2 * source + side
-            pl.when(at >= source)(lambda: gone(UP, panel, origin))
-            pl.when(at <= source)(lambda: gone(DOWN, panel, origin))
-            pl.when(goes_across(panel, jnp.int32(source)))(lambda: gone(ACROSS, panel, origin))
-    pl.when(at % 2 == 0)(lambda: gone(UP, last, 2 * at + 1 - side))
-    pl.when(at % 2 == 1)(lambda: gone(DOWN, last, 2 * at + 1 - side))
-    pl.when(row < rows - 1)(lambda: tail_copy().wait_send())
-    for step in range(1, rows):
-        pack_copy(step).wait_send()
+            pl.when((at >= source) & (at < line - 1))(lambda: corner_copy(UP, origin).wait_send())
+            pl.when((at <= source) & (at > 0))(lambda: corner_copy(DOWN, origin).wait_send())
+            corner_copy(ACROSS, origin).wait_send()
+
+    for step in range(steps):
+        move = row_copy(late, late_got.at[step], late_send.at[step], late_recv.at[step], step)
+        move.start()
+        if step == steps - 1:
+            all_gone()
+        move.wait()
+        late[...] += late_got[step]
+    down = lax.broadcasted_iota(jnp.int32, (late_width, width), 0)
+    over = lax.broadcasted_iota(jnp.int32, (late_width, width), 1)
+    turn = jnp.where(down + early_width == over, 1.0, 0.0).astype(F32)
+    turned = precise_dot(late[...], turn, (((0,), (0,)), ((), ())))
+    gram = jnp.concatenate(
+        [sums[1, columns : columns + early_width, :] + turned[:early_width], late[:, :width]], axis=0
+    )
+    coef_ref[...] = solved(gram, sums[1, :columns, :] + turned[width:], inverse)
 
 
 def finish_kernel(eig_ref, wall_ref, coef_ref, out_ref, held, sems):
@@ -445,10 +588,11 @@
         return pltpu.make_async_copy(held.at[:, cut(index)], out_ref.at[:, cut(index)], sems.at[index])
 
     coeffs = coef_ref[...]
+    order = last_order(cols, lax.axis_index("col"))
 
     @pl.loop(0, chunks)
     def _(index):
-        reflect = jnp.concatenate([wall_ref[part, :, cut(index)] for part in range(cols)], axis=0)
+        reflect = jnp.concatenate([wall_ref[part, :, cut(index)] for part in order], axis=0)
         update = lax.dot_general(coeffs, reflect, INNER, preferred_element_type=F32)
         held[:, cut(index)] = eig_ref[:, cut(index)] - update
         copy(index).start()
@@ -467,6 +611,7 @@
     width = width_own * cols
     steps = rows.bit_length() - 1
     chunks = rows_dev // tile_of(rows_dev, 14)
+    late_width = 2 * width_own
     vmem = pltpu.VMEM
     dma = pltpu.SemaphoreType.DMA
     eigen, wall, coeffs = pl.pallas_call(
@@ -476,24 +621,25 @@
             vmem((cols, width_own, rows_dev), BF16),
             vmem((columns, width), BF16),
         ),
-        in_specs=[
-            pl.BlockSpec(memory_space=pltpu.HBM),
-            pl.BlockSpec(memory_space=pltpu.VMEM),
-            pl.BlockSpec(memory_space=pltpu.SMEM),
-            pl.BlockSpec(memory_space=pltpu.HBM),
-        ],
+        in_specs=[pl.BlockSpec(memory_space=pltpu.HBM)] * 4,
         out_specs=[pl.BlockSpec(memory_space=pltpu.VMEM)] * 3,
         scratch_shapes=[
             vmem((cols, width_own, rows_dev), BF16),
+            vmem(span_vectors.shape, F32),
+            pltpu.SMEM(span_offsets.shape, jnp.int32),
             vmem((own, LANES), F32),
             vmem((own, LANES), F32),
             vmem((own, LANES), jnp.int32),
             vmem((own, LANES), F32),
             vmem((own, LANES), F32),
-            vmem((rows, columns + 2 * own, 2 * own), F32),
+            vmem((rows, columns + 2 * own + width_own, 2 * own), F32),
             vmem((count, columns + width, width), F32),
             vmem((count, steps, columns + width, width), F32),
-            dma,
+            vmem((late_width, columns + width), F32),
+            vmem((steps, late_width, columns + width), F32),
+            vmem((cols, 8, LANES), F32),
+            vmem((2, width, width), jnp.int32),
+            dma((3,)),
             dma((count,)),
             dma((count, cols, chunks)),
             dma((3, count, cols)),
@@ -502,6 +648,10 @@
             dma((rows,)),
             dma((count, steps)),
             dma((count, steps)),
+            dma((steps,)),
+            dma((steps,)),
+            dma((3, cols)),
+            dma((cols,)),
         ],
         compiler_params=pltpu.CompilerParams(
             collective_id=0, has_side_effects=True, vmem_limit_bytes=40 * 2**20
@@ -511,7 +661,7 @@
             bytes_accessed=8 * rows_dev * columns + 8 * width * rows_dev,
             transcendentals=0,
         ),
-    )(eigvecs, span_vectors, span_offsets, panels)
+    )(*(pltpu.with_memory_space_constraint(value, pltpu.HBM) for value in (eigvecs, span_vectors, span_offsets, panels)))
     return pl.pallas_call(
         finish_kernel,
         out_shape=jax.ShapeDtypeStruct(eigvecs.shape, F32),

time: 155 us -> 141 us (0.910)
  Pallas kernels: 152 us -> 141 us
  local copies, waits for them, and re-layouts: 2.85 us -> 0 us
    pallas_call x1, Pallas kernels: 149 us -> 138 us  [local(): pl.pallas_call(kernel, out_shape=(vmem(eigvecs.shape, F32), vmem((cols, w...]
    unnamed x6 -> x0, local copies, waits for them, and re-layouts: 2.85 us -> none
where the time goes in v2:
time: 141 us
  Pallas kernels  141 us (100%)
    pallas_call x1, Pallas kernels, local(): pl.pallas_call(kernel, out_shape=(vmem(eigvecs.shape, F32), vmem((cols, w...  138 us
    pallas_call x1, Pallas kernels, local(): pl.pallas_call(finish_kernel, out_shape=jax.ShapeDtypeStruct(eigvecs.shap...  3.1 us

profile of v2, /device:TPU:0, one launch (start us, length us, event | category | flops | bytes accessed | tf_op | source)
XLA Modules:
  0.0 141.3 jit_solution(3763850535451111454)
XLA Ops:
  0.0 138.0 %shard_map.46 = (f32[128,12544]{1,0:T(8,128)S(1)}, bf16[8,32,12544]{2,1,0:T(8,128)(2,1)S(1)}, bf16[128,256]{1,0:T(8,128)(2,1)S(1)}) custom-call(f32[128,12544]{1,0:T(8,128)} %eig_ref.1, f32[2,8,4,128]{3,2,1,0:T(4,128)} %vec_ref.1, s32[2,8]{1,0:T(2,128)} %off_ref.1, bf16[2,32,12544]{2,1,0:T(8,128)(2,1)} %pan_ref.1), custom_call_target="tpu_custom_call" | custom-call | flops 9865003008 | bytes 38535168 | tf_op jit(solution)/shard_map/pallas_call | solution.py:617
  138.0 3.1 %shard_map.47 = f32[128,12544]{1,0:T(8,128)} custom-call(f32[128,12544]{1,0:T(8,128)S(1)} %get-tuple-element.8.eig_ref, bf16[8,32,12544]{2,1,0:T(8,128)(2,1)S(1)} %get-tuple-element.9.wall_ref, bf16[128,256]{1,0:T(8,128)(2,1)S(1)} %get-tuple-element.10.coef_ref), custom_call_target="tpu_custom_call" | custom-call | flops 822083584 | bytes 12845056 | tf_op jit(solution)/shard_map/pallas_call | solution.py:665

commit v3 on v2

--- a/solution.py
+++ b/solution.py
@@ -54,8 +54,11 @@
     return inverse
 
 
-def last_order(cols, col):
-    line, at, side = cols // 2, col // 2, col % 2
+def natural_order(line):
+    return [(side, place) for place in range(line) for side in range(2)]
+
+
+def last_order(line, at, side):
     beside = at + 1 - 2 * (at % 2)
     far = (line - 1) * (1 - 2 * at // line)
     first, second = jnp.minimum(beside, far), jnp.maximum(beside, far)
@@ -63,15 +66,17 @@
     for index in range(line - 2):
         place = index + jnp.where(first <= index, 1, 0)
         early.append(place + jnp.where(second <= place, 1, 0))
-    order = [2 * place + side for place in range(line)]
-    return order + [2 * place + 1 - side for place in (*early, beside, far)]
+    order = [(side, place) for place in range(line)]
+    return order + [(1 - side, place) for place in (*early, beside, far)]
 
 
 def kernel(
     eig_ref, vec_ref, off_ref, pan_ref, eig, wall_last, coef_ref,
-    wall_first, vecs, offs, low, high, base, tail_out, tail_in, pack, sums, got, late, late_got, corner, places,
-    load_sem, own_sem, recv_sem, send_sem, tail_sem, pack_send, pack_recv, sum_send, sum_recv,
-    late_send, late_recv, corner_send, corner_recv,
+    wall_first, vecs, offs, low, high, base, tail_out, tail_in, pack, sums, got,
+    late, late_got, late_cast, late_cast_got, corner, places, blocks,
+    load_sem, own_sem, line_sem, first_sem, partner_sem, early_sem, last_sem, send_sem,
+    tail_sem, pack_send, pack_recv, sum_send, sum_recv, late_send, late_recv,
+    corner_send, corner_recv, corner_across,
 ):
     rows, cols = lax.axis_size("row"), lax.axis_size("col")
     line = cols // 2
@@ -91,34 +96,32 @@
     groups = rows_dev // group
     last = panels - 1
     beside = at + 1 - 2 * (at % 2)
-    order = last_order(cols, col)
+    far = (line - 1) * (1 - 2 * at // line)
+    other = 1 - side
+    natural, order = natural_order(line), last_order(line, at, side)
     late_width = 2 * width_own
     early_width = width - late_width
     fold = width_own // 8
+    bounds = (0, (chunks + 1) // 2, chunks)
 
     def cut(index):
         return pl.ds(pl.multiple_of(index * chunk, chunk), chunk)
+
+    short = max(1, chunk // LANES // 4) * LANES
+    closing = (
+        pl.ds(rows_dev - chunk, chunk - short),
+        pl.ds(rows_dev - short, short),
+    )
+
+    def span_of(part):
+        return pl.ds(bounds[part] * chunk, (bounds[part + 1] - bounds[part]) * chunk)
 
     def target(way):
         if way == ACROSS:
             return {"col": col + 1 - 2 * side}
         return {"col": col + 2 if way == UP else col - 2}
 
-    def copy(way, panel, origin, index, mine=False):
-        where = walls[panel].at[origin, :, cut(index)]
-        return pltpu.make_async_remote_copy(
-            src_ref=pan_ref.at[panel, :, cut(index)] if mine else where,
-            dst_ref=where,
-            send_sem=send_sem.at[way, panel, origin],
-            recv_sem=recv_sem.at[panel, origin, index],
-            device_id=target(way),
-            device_id_type=pl.DeviceIdType.MESH,
-        )
-
-    def send(way, panel, origin, index, mine=False):
-        def start():
-            copy(way, panel, origin, index, mine).start()
-
+    def guarded(way, start):
         if way == UP:
             pl.when(at < line - 1)(start)
         elif way == DOWN:
@@ -126,34 +129,66 @@
         else:
             start()
 
+    def copy(way, panel, piece, where, sem, mine=False):
+        dest = walls[panel].at[piece[0], piece[1], :, where]
+        return pltpu.make_async_remote_copy(
+            src_ref=pan_ref.at[panel, :, where] if mine else dest,
+            dst_ref=dest,
+            send_sem=send_sem.at[way, panel],
+            recv_sem=sem,
+            device_id=target(way),
+            device_id_type=pl.DeviceIdType.MESH,
+        )
+
+    def send(way, panel, piece, where, sem, mine=False):
+        guarded(way, lambda: copy(way, panel, piece, where, sem, mine).start())
+
+    def arrived(panel, ref, sem):
+        pltpu.make_async_remote_copy(
+            src_ref=ref, dst_ref=ref, send_sem=send_sem.at[ACROSS, panel], recv_sem=sem,
+            device_id=target(ACROSS), device_id_type=pl.DeviceIdType.MESH,
+        ).wait_recv()
+
     def send_own(way, panel):
-        @pl.loop(0, chunks)
+        for part in range(2):
+            if way == ACROSS:
+                sem = partner_sem.at[part] if panel == last else first_sem.at[part]
+            else:
+                sem = line_sem.at[panel, at, part]
+            send(way, panel, (side, at), span_of(part), sem, True)
+
+    def send_last(way, piece, part):
+        @pl.loop(bounds[part], min(bounds[part + 1], chunks - 1))
         def _(index):
-            send(way, panel, col, index, True)
-
-    def arrived(panel, origin, index):
-        copy(ACROSS, panel, origin, index).wait_recv()
-
-    def goes_across(panel, origin_at):
-        return (origin_at != beside) if panel == last else (origin_at >= 0)
-
-    def serve(panel, step, index):
+            send(way, last, piece, cut(index), last_sem.at[index])
+
+        if bounds[part + 1] == chunks:
+            for index, where in enumerate(closing):
+                send(way, last, piece, where, last_sem.at[chunks - 1 + index])
+
+    def serve(panel, step, part):
         for way, source in ((UP, at - step), (DOWN, at + step)):
             @pl.when((source >= 0) & (source < line))
             def _(way=way, source=source):
-                origin = 2 * source + side
-                arrived(panel, origin, index)
-                send(way, panel, origin, index)
-
-                @pl.when(goes_across(panel, source))
+                piece = (side, source)
+                sem = line_sem.at[panel, source, part]
+                arrived(panel, walls[panel].at[side, source, :, span_of(part)], sem)
+                send(way, panel, piece, span_of(part), sem)
+                if panel < last:
+                    send(ACROSS, panel, piece, span_of(part), first_sem.at[part])
+                    return
+
+                @pl.when(source == far)
                 def _():
-                    send(ACROSS, panel, origin, index)
+                    send_last(ACROSS, piece, part)
+
+                @pl.when((source != far) & (source != beside))
+                def _():
+                    send(ACROSS, panel, piece, span_of(part), early_sem.at[part])
 
     def serve_all(panel, step):
-        @pl.loop(0, chunks)
-        def _(index):
-            serve(panel, step, index)
-
+        for part in range(2):
+            serve(panel, step, part)
         if panel < last:
             @pl.when(at == step)
             def _():
@@ -163,17 +198,12 @@
             def _():
                 send_own(DOWN, panel + 1)
 
-    def serve_partner(index):
-        origin = 2 * at + 1 - side
-        arrived(last, origin, index)
-
-        @pl.when(at % 2 == 0)
-        def _():
-            send(UP, last, origin, index)
-
-        @pl.when(at % 2 == 1)
-        def _():
-            send(DOWN, last, origin, index)
+    def serve_partner(part):
+        arrived(last, walls[last].at[other, at, :, span_of(part)], partner_sem.at[part])
+        for way in (UP, DOWN):
+            @pl.when(at % 2 == way)
+            def _(way=way):
+                send_last(way, (other, at), part)
 
     vec_load = pltpu.make_async_copy(vec_ref, vecs, load_sem.at[1])
     off_load = pltpu.make_async_copy(off_ref, offs, load_sem.at[2])
@@ -199,7 +229,7 @@
     load = pltpu.make_async_copy(eig_ref, eig, load_sem.at[0])
     load.start()
     for panel in range(panels):
-        pltpu.make_async_copy(pan_ref.at[panel], walls[panel].at[col], own_sem.at[panel]).start()
+        pltpu.make_async_copy(pan_ref.at[panel], walls[panel].at[side, at], own_sem.at[panel]).start()
     pl.when(at == 0)(lambda: send_own(UP, 1))
     pl.when(at == line - 1)(lambda: send_own(DOWN, 1))
 
@@ -247,10 +277,10 @@
 
     pl.when(row < rows - 1)(lambda: tail_copy().start())
     for panel in range(panels):
-        pltpu.make_async_copy(pan_ref.at[panel], walls[panel].at[col], own_sem.at[panel]).wait()
+        pltpu.make_async_copy(pan_ref.at[panel], walls[panel].at[side, at], own_sem.at[panel]).wait()
 
     def own_products(index, acc):
-        mine = walls[last][col, :, cut(index)]
+        mine = walls[last][side, at, :, cut(index)]
         padded = jnp.concatenate([mine, jnp.zeros((LANES - width_own, chunk), BF16)], axis=0)
         return acc + lax.dot_general(mine, padded, LAST, preferred_element_type=F32)
 
@@ -285,22 +315,21 @@
 
     def pack_copy(step):
         return pltpu.make_async_remote_copy(
-            src_ref=pack.at[row], dst_ref=pack.at[row], send_sem=pack_send.at[step], recv_sem=pack_recv.at[row],
+            src_ref=pack.at[row], dst_ref=pack.at[row], send_sem=pack_send, recv_sem=pack_recv,
             device_id={"row": lax.rem(row + step, rows)}, device_id_type=pl.DeviceIdType.MESH,
         )
 
-    def pack_taken(step):
-        source = lax.rem(row + step, rows)
+    def pack_others():
+        ref = pack.at[pl.ds(0, rows - 1)]
         return pltpu.make_async_remote_copy(
-            src_ref=pack.at[source], dst_ref=pack.at[source], send_sem=pack_send.at[step], recv_sem=pack_recv.at[source],
-            device_id={"row": source}, device_id_type=pl.DeviceIdType.MESH,
+            src_ref=ref, dst_ref=ref, send_sem=pack_send, recv_sem=pack_recv,
+            device_id={"row": lax.rem(row + 1, rows)}, device_id_type=pl.DeviceIdType.MESH,
         )
 
     for step in range(1, rows):
         pack_copy(step).start()
-    serve_all(0, 1) if line > 1 else None
-    for step in range(1, rows):
-        pack_taken(step).wait_recv()
+    serve_all(0, 1)
+    pack_others().wait_recv()
 
     square = pack[0, columns + 2 * own :, :]
     for index in range(1, rows):
@@ -314,37 +343,33 @@
     folded = square[:8]
     for index in range(1, fold):
         folded = folded + pltpu.roll(square[8 * index : 8 * index + 8], index * width_own, 1)
-    corner[col] = folded
-
-    def corner_copy(way, origin):
-        return pltpu.make_async_remote_copy(
-            src_ref=corner.at[origin], dst_ref=corner.at[origin],
-            send_sem=corner_send.at[way, origin], recv_sem=corner_recv.at[origin],
+    corner[side, at] = folded
+
+    def send_corner(way, source):
+        ref = corner.at[side, source]
+        move = pltpu.make_async_remote_copy(
+            src_ref=ref, dst_ref=ref, send_sem=corner_send.at[way],
+            recv_sem=corner_across if way == ACROSS else corner_recv.at[source],
             device_id=target(way), device_id_type=pl.DeviceIdType.MESH,
         )
-
-    def send_corner(way, origin):
-        def start():
-            corner_copy(way, origin).start()
-
-        if way == UP:
-            pl.when(at < line - 1)(start)
-        elif way == DOWN:
-            pl.when(at > 0)(start)
-        else:
-            start()
+        guarded(way, move.start)
+
+    def corner_wait(ref, way, sem):
+        return pltpu.make_async_remote_copy(
+            src_ref=ref, dst_ref=ref, send_sem=corner_send.at[way], recv_sem=sem,
+            device_id=target(way), device_id_type=pl.DeviceIdType.MESH,
+        )
 
     def serve_corner(step):
         for way, source in ((UP, at - step), (DOWN, at + step)):
             @pl.when((source >= 0) & (source < line))
             def _(way=way, source=source):
-                origin = 2 * source + side
-                corner_copy(way, origin).wait_recv()
-                send_corner(way, origin)
-                send_corner(ACROSS, origin)
+                corner_wait(corner.at[side, source], ACROSS, corner_recv.at[source]).wait_recv()
+                send_corner(way, source)
+                send_corner(ACROSS, source)
 
     for way in (UP, DOWN, ACROSS):
-        send_corner(way, col)
+        send_corner(way, at)
 
     def placed(value, shift):
         wide = value
@@ -355,14 +380,14 @@
         return pltpu.roll(wide, shift, 1) if shift else wide
 
     inner = jnp.zeros((columns, total), F32)
-    blocks = []
+    bands = []
     for index in range(rows):
         inner = inner + placed(pack[index, :columns, :], index - 1)
         block = placed(pack[index, columns : columns + own, :], index - 1)
         if index < rows - 1:
             block = block + placed(pack[index + 1, columns + own : columns + 2 * own, :], index + 1)
-        blocks.append(block)
-    matrix = jnp.concatenate(blocks, axis=0)
+        bands.append(block)
+    matrix = jnp.concatenate(bands, axis=0)
     orders = []
     for axis in range(2):
         value = lax.broadcasted_iota(jnp.int32, (total, total), axis)
@@ -385,17 +410,16 @@
         eig[:, cut_group(index)] -= dot_split(coeffs, halves(right), INNER)
 
     eig[:, :LANES] -= dot_split(coeffs, halves(jnp.concatenate([before, nothing], axis=0)), INNER)
-    if line > 2:
-        serve_all(0, line - 1)
+    serve_all(0, line - 1)
     serve_corner(1)
     for panel in range(1, panels):
         send_own(ACROSS, panel)
 
-    def reflectors(panel, index, parts):
-        return jnp.concatenate([walls[panel][part, :, cut(index)] for part in parts], axis=0)
-
-    def rounded(index):
-        return eig[:, cut(index)].astype(BF16)
+    def reflectors(panel, where, parts):
+        return jnp.concatenate([walls[panel][part[0], part[1], :, where] for part in parts], axis=0)
+
+    def rounded(where):
+        return eig[:, where].astype(BF16)
 
     def row_copy(source, dest, send, recv, step):
         bit = 2**step
@@ -430,7 +454,7 @@
     def diagonal(parts):
         stack = []
         for part in parts:
-            folded = corner[part]
+            folded = corner[part[0], part[1]]
             stack.append(folded)
             for index in range(1, fold):
                 stack.append(pltpu.roll(folded, LANES - index * width_own, 1))
@@ -447,46 +471,53 @@
             part_at = lax.broadcasted_iota(jnp.int32, (width, width), axis) // width_own
             place = jnp.zeros_like(part_at)
             for index, part in enumerate(parts):
-                place = jnp.where(part_at == index, part, place)
+                place = jnp.where(part_at == index, 2 * part[1] + part[0], place)
             places[axis] = place
 
     def solved(gram, inner, inverse):
-        size = 1
+        down, over = places[0], places[1]
+        if cols > 8:
+            size = 1
+            while size < cols:
+                off = (down // (2 * size) == over // (2 * size)) & (down // size < over // size)
+                off = halves(jnp.where(off, gram, 0.0))
+                split = halves(inverse)
+                inverse = inverse - dot_split(split, halves(dot_split(off, split, INNER)), INNER)
+                size *= 2
+            return dot_split(halves(inner), halves(inverse), LAST).astype(BF16)
+        split = halves(inverse)
+        power = halves(dot_split(split, halves(jnp.where(down < over, gram, 0.0)), INNER))
+        value = dot_split(halves(inner), split, LAST)
+        value = value - dot_split(halves(value), power, LAST)
+        size = 2
         while size < cols:
-            down, over = places[0], places[1]
-            off = (down // (2 * size) == over // (2 * size)) & (down // size < over // size)
-            off = halves(jnp.where(off, gram, 0.0))
-            split = halves(inverse)
-            inverse = inverse - dot_split(split, halves(dot_split(off, split, INNER)), INNER)
+            power = halves(dot_split(power, power, INNER))
+            value = value + dot_split(halves(value), power, LAST)
             size *= 2
-        return dot_split(halves(inner), halves(inverse), LAST).astype(BF16)
+        return value.astype(BF16)
 
     for panel in range(panels):
         sums[panel] = jnp.zeros_like(sums[panel])
     late[...] = jnp.zeros_like(late)
-    natural = list(range(cols))
-
-    @pl.loop(0, chunks)
-    def _(index):
-        for source in range(line):
-            arrived(0, 2 * source + 1 - side, index)
-        reflect = reflectors(0, index, natural)
-        left = jnp.concatenate([rounded(index), reflect], axis=0)
-        sums[0] += lax.dot_general(left, reflect, LAST, preferred_element_type=F32)
-        serve(1, 1, index)
+    for part in range(2):
+        arrived(0, walls[0].at[other, :, :, span_of(part)], first_sem.at[part])
+
+        @pl.loop(bounds[part], bounds[part + 1])
+        def _(index):
+            reflect = reflectors(0, cut(index), natural)
+            left = jnp.concatenate([rounded(cut(index)), reflect], axis=0)
+            sums[0] += lax.dot_general(left, reflect, LAST, preferred_element_type=F32)
+
+        serve(1, 1, part)
 
     def serve_between():
         for step in range(2, line - 1):
-            @pl.loop(0, chunks)
-            def _(index):
-                serve(1, step, index)
-
-        @pl.loop(0, chunks)
-        def _(index):
-            serve_partner(index)
-
-    if line > 2:
-        serve_corner(2)
+            for part in range(2):
+                serve(1, step, part)
+        for part in range(2):
+            serve_partner(part)
+
+    serve_corner(2)
     row_sum(0, serve_between)
     for step in range(3, line):
         serve_corner(step)
@@ -494,89 +525,96 @@
 
     @pl.loop(0, chunks)
     def _(index):
-        reflect = reflectors(0, index, natural)
+        reflect = reflectors(0, cut(index), natural)
         eig[:, cut(index)] -= lax.dot_general(coeffs, reflect, INNER, preferred_element_type=F32)
 
     early_parts, late_parts = order[:-2], order[-2:]
 
-    @pl.loop(0, chunks)
-    def _(index):
-        serve(1, line - 1, index)
-        for source in range(line):
-            other = 2 * source + 1 - side
-            known = (at == source) | (late_parts[0] == other) | (late_parts[1] == other)
-            pl.when(jnp.logical_not(known))(lambda: arrived(1, other, index))
-        reflect = reflectors(1, index, early_parts)
-        left = jnp.concatenate([rounded(index), reflect], axis=0)
-        right = jnp.concatenate([reflect, jnp.zeros((late_width, chunk), BF16)], axis=0)
-        sums[1, pl.ds(0, kept[1]), :] += lax.dot_general(left, right, LAST, preferred_element_type=F32)
-
-    def add_late(index):
-        for part in late_parts:
-            arrived(1, part, index)
-        reflect = reflectors(1, index, late_parts)
-        right = jnp.concatenate([reflectors(1, index, order), rounded(index)], axis=0)
+    for part in range(2):
+        serve(1, line - 1, part)
+        arrived(1, walls[1].at[other, pl.ds(0, line - 3), :, span_of(part)], early_sem.at[part])
+
+        @pl.loop(bounds[part], bounds[part + 1])
+        def _(index):
+            reflect = reflectors(1, cut(index), early_parts)
+            left = jnp.concatenate([rounded(cut(index)), reflect], axis=0)
+            right = jnp.concatenate([reflect, jnp.zeros((late_width, chunk), BF16)], axis=0)
+            sums[1, pl.ds(0, kept[1]), :] += lax.dot_general(left, right, LAST, preferred_element_type=F32)
+
+    def add_late(where, sem):
+        arrived(1, walls[1].at[other, pl.ds(0, 2), :, where], sem)
+        reflect = reflectors(1, where, late_parts)
+        right = jnp.concatenate([reflectors(1, where, order), rounded(where)], axis=0)
         late[...] += lax.dot_general(reflect, right, LAST, preferred_element_type=F32)
 
-    for source in range(line):
-        corner_copy(ACROSS, 2 * source + 1 - side).wait_recv()
-    set_places(order)
-    row_sum(1, lambda: pl.loop(0, chunks - 1)(add_late))
-    inverse = diagonal(order)
-    add_late(chunks - 1)
-    def gone(way, panel, origin):
-        def wait():
-            piece = walls[panel].at[origin]
-            pltpu.make_async_remote_copy(
-                src_ref=piece, dst_ref=piece, send_sem=send_sem.at[way, panel, origin],
-                recv_sem=recv_sem.at[panel, origin, 0], device_id=target(way),
-                device_id_type=pl.DeviceIdType.MESH,
-            ).wait_send()
-
-        if way == UP:
-            pl.when(at < line - 1)(wait)
-        elif way == DOWN:
-            pl.when(at > 0)(wait)
-        else:
-            wait()
+    def prepare():
+        corner_wait(corner.at[other], ACROSS, corner_across).wait_recv()
+        set_places(order)
+        blocks[...] = diagonal(order)
+        pl.loop(0, max(chunks - 2, 0))(lambda index: add_late(cut(index), last_sem.at[index]))
+
+    row_sum(1, prepare)
+    for index in range(max(chunks - 2, 0), chunks - 1):
+        add_late(cut(index), last_sem.at[index])
+    for index, where in enumerate(closing):
+        add_late(where, last_sem.at[chunks - 1 + index])
+
+    def gone(ref, way, sem):
+        pltpu.make_async_remote_copy(
+            src_ref=ref, dst_ref=ref, send_sem=sem, recv_sem=partner_sem.at[0], device_id=target(way),
+            device_id_type=pl.DeviceIdType.MESH,
+        ).wait_send()
 
     def all_gone():
         for panel in range(panels):
-            for source in range(line):
-                origin = 2 * source + side
-                pl.when(at >= source)(lambda: gone(UP, panel, origin))
-                pl.when(at <= source)(lambda: gone(DOWN, panel, origin))
-                pl.when(goes_across(panel, jnp.int32(source)))(lambda: gone(ACROSS, panel, origin))
-        pl.when(at % 2 == 0)(lambda: gone(UP, last, 2 * at + 1 - side))
-        pl.when(at % 2 == 1)(lambda: gone(DOWN, last, 2 * at + 1 - side))
+            pieces = walls[panel].at[0]
+            for place in range(line):
+                @pl.when(at == place)
+                def _(place=place):
+                    above, below = place + 1, line - place
+                    if panel == last:
+                        above, below = above + 1 - place % 2, below + place % 2
+                    if place < line - 1:
+                        gone(pieces.at[pl.ds(0, above)], UP, send_sem.at[UP, panel])
+                    if place > 0:
+                        gone(pieces.at[pl.ds(0, below)], DOWN, send_sem.at[DOWN, panel])
+            count = line - 1 if panel == last else line
+            gone(pieces.at[pl.ds(0, count)], ACROSS, send_sem.at[ACROSS, panel])
+        for place in range(line):
+            @pl.when(at == place)
+            def _(place=place):
+                if place < line - 1:
+                    corner_wait(corner.at[0, pl.ds(0, place + 1)], UP, corner_across).wait_send()
+                if place > 0:
+                    corner_wait(corner.at[0, pl.ds(0, line - place)], DOWN, corner_across).wait_send()
+        corner_wait(corner.at[0], ACROSS, corner_across).wait_send()
         pl.when(row < rows - 1)(lambda: tail_copy().wait_send())
-        for step in range(1, rows):
-            pack_copy(step).wait_send()
-        for source in range(line):
-            origin = 2 * source + side
-            pl.when((at >= source) & (at < line - 1))(lambda: corner_copy(UP, origin).wait_send())
-            pl.when((at <= source) & (at > 0))(lambda: corner_copy(DOWN, origin).wait_send())
-            corner_copy(ACROSS, origin).wait_send()
+        pack_others().wait_send()
 
     for step in range(steps):
-        move = row_copy(late, late_got.at[step], late_send.at[step], late_recv.at[step], step)
+        if step == 0:
+            move = row_copy(late, late_got, late_send.at[step], late_recv.at[step], step)
+        else:
+            late_cast[...] = late[...].astype(BF16)
+            move = row_copy(late_cast, late_cast_got.at[step - 1], late_send.at[step], late_recv.at[step], step)
         move.start()
         if step == steps - 1:
             all_gone()
         move.wait()
-        late[...] += late_got[step]
+        late[...] += late_got[...] if step == 0 else late_cast_got[step - 1].astype(F32)
     down = lax.broadcasted_iota(jnp.int32, (late_width, width), 0)
     over = lax.broadcasted_iota(jnp.int32, (late_width, width), 1)
-    turn = jnp.where(down + early_width == over, 1.0, 0.0).astype(F32)
-    turned = precise_dot(late[...], turn, (((0,), (0,)), ((), ())))
+    turn = jnp.where(down + early_width == over, 1.0, 0.0).astype(BF16)
+    first_dim = (((0,), (0,)), ((), ()))
+    turned = sum(lax.dot_general(part, turn, first_dim, preferred_element_type=F32) for part in halves(late[...]))
     gram = jnp.concatenate(
         [sums[1, columns : columns + early_width, :] + turned[:early_width], late[:, :width]], axis=0
     )
-    coef_ref[...] = solved(gram, sums[1, :columns, :] + turned[width:], inverse)
+    coef_ref[...] = solved(gram, sums[1, :columns, :] + turned[width:], blocks[...])
 
 
 def finish_kernel(eig_ref, wall_ref, coef_ref, out_ref, held, sems):
-    cols = wall_ref.shape[0]
+    line = wall_ref.shape[1]
     rows_dev = eig_ref.shape[1]
     chunk = tile_of(rows_dev, 14)
     chunks = rows_dev // chunk
@@ -588,11 +626,11 @@
         return pltpu.make_async_copy(held.at[:, cut(index)], out_ref.at[:, cut(index)], sems.at[index])
 
     coeffs = coef_ref[...]
-    order = last_order(cols, lax.axis_index("col"))
-
-    @pl.loop(0, chunks)
-    def _(index):
-        reflect = jnp.concatenate([wall_ref[part, :, cut(index)] for part in order], axis=0)
+    col = lax.axis_index("col")
+    order = last_order(line, col // 2, col % 2)
+
+    for index in range(chunks):
+        reflect = jnp.concatenate([wall_ref[part[0], part[1], :, cut(index)] for part in order], axis=0)
         update = lax.dot_general(coeffs, reflect, INNER, preferred_element_type=F32)
         held[:, cut(index)] = eig_ref[:, cut(index)] - update
         copy(index).start()
@@ -612,19 +650,20 @@
     steps = rows.bit_length() - 1
     chunks = rows_dev // tile_of(rows_dev, 14)
     late_width = 2 * width_own
+    line = cols // 2
     vmem = pltpu.VMEM
     dma = pltpu.SemaphoreType.DMA
     eigen, wall, coeffs = pl.pallas_call(
         kernel,
         out_shape=(
             vmem(eigvecs.shape, F32),
-            vmem((cols, width_own, rows_dev), BF16),
+            vmem((2, line, width_own, rows_dev), BF16),
             vmem((columns, width), BF16),
         ),
         in_specs=[pl.BlockSpec(memory_space=pltpu.HBM)] * 4,
         out_specs=[pl.BlockSpec(memory_space=pltpu.VMEM)] * 3,
         scratch_shapes=[
-            vmem((cols, width_own, rows_dev), BF16),
+            vmem((2, line, width_own, rows_dev), BF16),
             vmem(span_vectors.shape, F32),
             pltpu.SMEM(span_offsets.shape, jnp.int32),
             vmem((own, LANES), F32),
@@ -636,22 +675,30 @@
             vmem((count, columns + width, width), F32),
             vmem((count, steps, columns + width, width), F32),
             vmem((late_width, columns + width), F32),
-            vmem((steps, late_width, columns + width), F32),
-            vmem((cols, 8, LANES), F32),
+            vmem((late_width, columns + width), F32),
+            vmem((late_width, columns + width), BF16),
+            vmem((steps, late_width, columns + width), BF16),
+            vmem((2, line, 8, LANES), F32),
             vmem((2, width, width), jnp.int32),
+            vmem((width, width), F32),
             dma((3,)),
             dma((count,)),
-            dma((count, cols, chunks)),
-            dma((3, count, cols)),
+            dma((count, line, 2)),
             dma((2,)),
-            dma((rows,)),
-            dma((rows,)),
+            dma((2,)),
+            dma((2,)),
+            dma((chunks + 1,)),
+            dma((3, count)),
+            dma((2,)),
+            dma,
+            dma,
             dma((count, steps)),
             dma((count, steps)),
             dma((steps,)),
             dma((steps,)),
-            dma((3, cols)),
-            dma((cols,)),
+            dma((3,)),
+            dma((line,)),
+            dma,
         ],
         compiler_params=pltpu.CompilerParams(
             collective_id=0, has_side_effects=True, vmem_limit_bytes=40 * 2**20
@@ -667,7 +714,7 @@
         out_shape=jax.ShapeDtypeStruct(eigvecs.shape, F32),
         in_specs=[pl.BlockSpec(memory_space=pltpu.VMEM)] * 3,
         out_specs=pl.BlockSpec(memory_space=pl.ANY),
-        scratch_shapes=[vmem(eigvecs.shape, F32), dma((chunks,))],
+        scratch_shapes=[vmem(eigvecs.shape, F32), dma((rows_dev // tile_of(rows_dev, 14),))],
         compiler_params=pltpu.CompilerParams(vmem_limit_bytes=16 * 2**20),
         cost_estimate=pl.CostEstimate(
             flops=2 * width * columns * rows_dev, bytes_accessed=8 * columns * rows_dev, transcendentals=0

time: 141 us -> 137 us (0.972)
  Pallas kernels: 141 us -> 137 us
    pallas_call x1, Pallas kernels: 138 us -> 133 us  [local(): pl.pallas_call(kernel, out_shape=(vmem(eigvecs.shape, F32), vmem((2, line...]
where the time goes in v3:
time: 137 us
  Pallas kernels  137 us (100%)
    pallas_call x1, Pallas kernels, local(): pl.pallas_call(kernel, out_shape=(vmem(eigvecs.shape, F32), vmem((2, line...  133 us
    pallas_call x1, Pallas kernels, local(): pl.pallas_call(finish_kernel, out_shape=jax.ShapeDtypeStruct(eigvecs.shap...  3.1 us

profile of v3, /device:TPU:0, one launch (start us, length us, event | category | flops | bytes accessed | tf_op | source)
XLA Modules:
  0.0 136.7 jit_solution(2978729402103168777)
XLA Ops:
  0.0 133.4 %shard_map.46 = (f32[128,12544]{1,0:T(8,128)S(1)}, bf16[2,4,32,12544]{3,2,1,0:T(8,128)(2,1)S(1)}, bf16[128,256]{1,0:T(8,128)(2,1)S(1)}) custom-call(f32[128,12544]{1,0:T(8,128)} %eig_ref.1, f32[2,8,4,128]{3,2,1,0:T(4,128)} %vec_ref.1, s32[2,8]{1,0:T(2,128)} %off_ref.1, bf16[2,32,12544]{2,1,0:T(8,128)(2,1)} %pan_ref.1), custom_call_target="tpu_custom_call" | custom-call | flops 9865003008 | bytes 38535168 | tf_op jit(solution)/shard_map/pallas_call | solution.py:656
  133.4 3.1 %shard_map.47 = f32[128,12544]{1,0:T(8,128)} custom-call(f32[128,12544]{1,0:T(8,128)S(1)} %get-tuple-element.8.eig_ref, bf16[2,4,32,12544]{3,2,1,0:T(8,128)(2,1)S(1)} %get-tuple-element.9.wall_ref, bf16[128,256]{1,0:T(8,128)(2,1)S(1)} %get-tuple-element.10.coef_ref), custom_call_target="tpu_custom_call" | custom-call | flops 822083584 | bytes 12845056 | tf_op jit(solution)/shard_map/pallas_call | solution.py:712

commit v4 on v3

--- a/solution.py
+++ b/solution.py
@@ -73,10 +73,10 @@
 def kernel(
     eig_ref, vec_ref, off_ref, pan_ref, eig, wall_last, coef_ref,
     wall_first, vecs, offs, low, high, base, tail_out, tail_in, pack, sums, got,
-    late, late_got, late_cast, late_cast_got, corner, places, blocks,
+    late, late_got, late_cast, late_cast_got, bulk, bulk_got, corner, places, blocks,
     load_sem, own_sem, line_sem, first_sem, partner_sem, early_sem, last_sem, send_sem,
     tail_sem, pack_send, pack_recv, sum_send, sum_recv, late_send, late_recv,
-    corner_send, corner_recv, corner_across,
+    bulk_send, bulk_recv, corner_send, corner_recv, corner_across,
 ):
     rows, cols = lax.axis_size("row"), lax.axis_size("col")
     line = cols // 2
@@ -499,6 +499,7 @@
     for panel in range(panels):
         sums[panel] = jnp.zeros_like(sums[panel])
     late[...] = jnp.zeros_like(late)
+    bulk[...] = jnp.zeros_like(bulk)
     for part in range(2):
         arrived(0, walls[0].at[other, :, :, span_of(part)], first_sem.at[part])
 
@@ -541,23 +542,31 @@
             right = jnp.concatenate([reflect, jnp.zeros((late_width, chunk), BF16)], axis=0)
             sums[1, pl.ds(0, kept[1]), :] += lax.dot_general(left, right, LAST, preferred_element_type=F32)
 
-    def add_late(where, sem):
+    def add_late(where, sem, into):
         arrived(1, walls[1].at[other, pl.ds(0, 2), :, where], sem)
         reflect = reflectors(1, where, late_parts)
         right = jnp.concatenate([reflectors(1, where, order), rounded(where)], axis=0)
-        late[...] += lax.dot_general(reflect, right, LAST, preferred_element_type=F32)
+        into[...] += lax.dot_general(reflect, right, LAST, preferred_element_type=F32)
 
     def prepare():
         corner_wait(corner.at[other], ACROSS, corner_across).wait_recv()
         set_places(order)
         blocks[...] = diagonal(order)
-        pl.loop(0, max(chunks - 2, 0))(lambda index: add_late(cut(index), last_sem.at[index]))
+        pl.loop(0, max(chunks - 2, 0))(lambda index: add_late(cut(index), last_sem.at[index], bulk))
 
     row_sum(1, prepare)
+    def bulk_move(step):
+        return row_copy(bulk, bulk_got.at[step], bulk_send.at[step], bulk_recv.at[step], step)
+
+    bulk_move(0).start()
     for index in range(max(chunks - 2, 0), chunks - 1):
-        add_late(cut(index), last_sem.at[index])
+        add_late(cut(index), last_sem.at[index], late)
+    for step in range(1, steps):
+        bulk_move(step - 1).wait()
+        bulk[...] += bulk_got[step - 1]
+        bulk_move(step).start()
     for index, where in enumerate(closing):
-        add_late(where, last_sem.at[chunks - 1 + index])
+        add_late(where, last_sem.at[chunks - 1 + index], late)
 
     def gone(ref, way, sem):
         pltpu.make_async_remote_copy(
@@ -600,15 +609,18 @@
         move.start()
         if step == steps - 1:
             all_gone()
+            bulk_move(step).wait()
+            bulk[...] += bulk_got[step]
         move.wait()
         late[...] += late_got[...] if step == 0 else late_cast_got[step - 1].astype(F32)
+    summed = late[...] + bulk[...]
     down = lax.broadcasted_iota(jnp.int32, (late_width, width), 0)
     over = lax.broadcasted_iota(jnp.int32, (late_width, width), 1)
     turn = jnp.where(down + early_width == over, 1.0, 0.0).astype(BF16)
     first_dim = (((0,), (0,)), ((), ()))
-    turned = sum(lax.dot_general(part, turn, first_dim, preferred_element_type=F32) for part in halves(late[...]))
+    turned = sum(lax.dot_general(part, turn, first_dim, preferred_element_type=F32) for part in halves(summed))
     gram = jnp.concatenate(
-        [sums[1, columns : columns + early_width, :] + turned[:early_width], late[:, :width]], axis=0
+        [sums[1, columns : columns + early_width, :] + turned[:early_width], summed[:, :width]], axis=0
     )
     coef_ref[...] = solved(gram, sums[1, :columns, :] + turned[width:], blocks[...])
 
@@ -678,6 +690,8 @@
             vmem((late_width, columns + width), F32),
             vmem((late_width, columns + width), BF16),
             vmem((steps, late_width, columns + width), BF16),
+            vmem((late_width, columns + width), F32),
+            vmem((steps, late_width, columns + width), F32),
             vmem((2, line, 8, LANES), F32),
             vmem((2, width, width), jnp.int32),
             vmem((width, width), F32),
@@ -694,6 +708,8 @@
             dma,
             dma((count, steps)),
             dma((count, steps)),
+            dma((steps,)),
+            dma((steps,)),
             dma((steps,)),
             dma((steps,)),
             dma((3,)),

time: 137 us -> 137 us (level)
  no operation moved by 1% of the time
where the time goes in v4:
time: 137 us
  Pallas kernels  137 us (100%)
    pallas_call x1, Pallas kernels, local(): pl.pallas_call(kernel, out_shape=(vmem(eigvecs.shape, F32), vmem((2, line...  133 us
    pallas_call x1, Pallas kernels, local(): pl.pallas_call(finish_kernel, out_shape=jax.ShapeDtypeStruct(eigvecs.shap...  3.1 us

profile of v4, /device:TPU:0, one launch (start us, length us, event | category | flops | bytes accessed | tf_op | source)
XLA Modules:
  0.0 136.7 jit_solution(2830268512191690044)
XLA Ops:
  0.0 133.5 %shard_map.46 = (f32[128,12544]{1,0:T(8,128)S(1)}, bf16[2,4,32,12544]{3,2,1,0:T(8,128)(2,1)S(1)}, bf16[128,256]{1,0:T(8,128)(2,1)S(1)}) custom-call(f32[128,12544]{1,0:T(8,128)} %eig_ref.1, f32[2,8,4,128]{3,2,1,0:T(4,128)} %vec_ref.1, s32[2,8]{1,0:T(2,128)} %off_ref.1, bf16[2,32,12544]{2,1,0:T(8,128)(2,1)} %pan_ref.1), custom_call_target="tpu_custom_call" | custom-call | flops 9865003008 | bytes 38535168 | tf_op jit(solution)/shard_map/pallas_call | solution.py:668
  133.5 3.1 %shard_map.47 = f32[128,12544]{1,0:T(8,128)} custom-call(f32[128,12544]{1,0:T(8,128)S(1)} %get-tuple-element.8.eig_ref, bf16[2,4,32,12544]{3,2,1,0:T(8,128)(2,1)S(1)} %get-tuple-element.9.wall_ref, bf16[128,256]{1,0:T(8,128)(2,1)S(1)} %get-tuple-element.10.coef_ref), custom_call_target="tpu_custom_call" | custom-call | flops 822083584 | bytes 12845056 | tf_op jit(solution)/shard_map/pallas_call | solution.py:728

commit v5 on v4

--- a/solution.py
+++ b/solution.py
@@ -207,8 +207,6 @@
 
     vec_load = pltpu.make_async_copy(vec_ref, vecs, load_sem.at[1])
     off_load = pltpu.make_async_copy(off_ref, offs, load_sem.at[2])
-    vec_load.start()
-    off_load.start()
 
     barrier = pltpu.get_barrier_semaphore()
 
@@ -220,6 +218,8 @@
     pl.when(at < line - 1)(lambda: greet(target(UP)))
     for step in range(1, rows):
         greet({"row": lax.rem(row + step, rows)})
+    vec_load.start()
+    off_load.start()
     neighbours = jnp.minimum(at, 1) + jnp.minimum(line - 1 - at, 1)
     pl.semaphore_wait(barrier, rows + neighbours)
 
@@ -437,7 +437,7 @@
         for step in range(steps):
             move = row_copy(
                 sums.at[panel, rows_at], got.at[panel, step, rows_at],
-                sum_send.at[panel, step], sum_recv.at[panel, step], step,
+                sum_send, sum_recv.at[panel, step], step,
             )
             move.start()
             if step == steps - 1:
@@ -556,7 +556,7 @@
 
     row_sum(1, prepare)
     def bulk_move(step):
-        return row_copy(bulk, bulk_got.at[step], bulk_send.at[step], bulk_recv.at[step], step)
+        return row_copy(bulk, bulk_got.at[step], bulk_send, bulk_recv.at[step], step)
 
     bulk_move(0).start()
     for index in range(max(chunks - 2, 0), chunks - 1):
@@ -602,10 +602,10 @@
 
     for step in range(steps):
         if step == 0:
-            move = row_copy(late, late_got, late_send.at[step], late_recv.at[step], step)
+            move = row_copy(late, late_got, late_send, late_recv.at[step], step)
         else:
             late_cast[...] = late[...].astype(BF16)
-            move = row_copy(late_cast, late_cast_got.at[step - 1], late_send.at[step], late_recv.at[step], step)
+            move = row_copy(late_cast, late_cast_got.at[step - 1], late_send, late_recv.at[step], step)
         move.start()
         if step == steps - 1:
             all_gone()
@@ -629,26 +629,25 @@
     line = wall_ref.shape[1]
     rows_dev = eig_ref.shape[1]
     chunk = tile_of(rows_dev, 14)
-    chunks = rows_dev // chunk
-
-    def cut(index):
-        return pl.ds(pl.multiple_of(index * chunk, chunk), chunk)
+    pieces, begin = [], 0
+    while begin < rows_dev:
+        size = min(chunk // 2 // LANES * LANES if not pieces else chunk, rows_dev - begin)
+        pieces.append(pl.ds(begin, size))
+        begin += size
 
     def copy(index):
-        return pltpu.make_async_copy(held.at[:, cut(index)], out_ref.at[:, cut(index)], sems.at[index])
+        where = pieces[index]
+        return pltpu.make_async_copy(held.at[:, where], out_ref.at[:, where], sems.at[index])
 
     coeffs = coef_ref[...]
     col = lax.axis_index("col")
     order = last_order(line, col // 2, col % 2)
-
-    for index in range(chunks):
-        reflect = jnp.concatenate([wall_ref[part[0], part[1], :, cut(index)] for part in order], axis=0)
+    for index, where in enumerate(pieces):
+        reflect = jnp.concatenate([wall_ref[part[0], part[1], :, where] for part in order], axis=0)
         update = lax.dot_general(coeffs, reflect, INNER, preferred_element_type=F32)
-        held[:, cut(index)] = eig_ref[:, cut(index)] - update
+        held[:, where] = eig_ref[:, where] - update
         copy(index).start()
-
-    @pl.loop(0, chunks)
-    def _(index):
+    for index in range(len(pieces)):
         copy(index).wait()
 
 
@@ -706,11 +705,11 @@
             dma((2,)),
             dma,
             dma,
+            dma,
             dma((count, steps)),
-            dma((count, steps)),
+            dma,
             dma((steps,)),
-            dma((steps,)),
-            dma((steps,)),
+            dma,
             dma((steps,)),
             dma((3,)),
             dma((line,)),
@@ -730,7 +729,7 @@
         out_shape=jax.ShapeDtypeStruct(eigvecs.shape, F32),
         in_specs=[pl.BlockSpec(memory_space=pltpu.VMEM)] * 3,
         out_specs=pl.BlockSpec(memory_space=pl.ANY),
-        scratch_shapes=[vmem(eigvecs.shape, F32), dma((rows_dev // tile_of(rows_dev, 14),))],
+        scratch_shapes=[vmem(eigvecs.shape, F32), dma((rows_dev // tile_of(rows_dev, 14) + 1,))],
         compiler_params=pltpu.CompilerParams(vmem_limit_bytes=16 * 2**20),
         cost_estimate=pl.CostEstimate(
             flops=2 * width * columns * rows_dev, bytes_accessed=8 * columns * rows_dev, transcendentals=0

time: 137 us -> 137 us (level)
  no operation moved by 1% of the time
where the time goes in v5:
time: 137 us
  Pallas kernels  136 us (99%)
    pallas_call x1, Pallas kernels, local(): pl.pallas_call(kernel, out_shape=(vmem(eigvecs.shape, F32), vmem((2, line...  133 us
    pallas_call x1, Pallas kernels, local(): pl.pallas_call(finish_kernel, out_shape=jax.ShapeDtypeStruct(eigvecs.shap...  3.03 us

profile of v5, /device:TPU:0, one launch (start us, length us, event | category | flops | bytes accessed | tf_op | source)
XLA Modules:
  0.0 136.6 jit_solution(14180026491955509913)
XLA Ops:
  0.0 133.4 %shard_map.46 = (f32[128,12544]{1,0:T(8,128)S(1)}, bf16[2,4,32,12544]{3,2,1,0:T(8,128)(2,1)S(1)}, bf16[128,256]{1,0:T(8,128)(2,1)S(1)}) custom-call(f32[128,12544]{1,0:T(8,128)} %eig_ref.1, f32[2,8,4,128]{3,2,1,0:T(4,128)} %vec_ref.1, s32[2,8]{1,0:T(2,128)} %off_ref.1, bf16[2,32,12544]{2,1,0:T(8,128)(2,1)} %pan_ref.1), custom_call_target="tpu_custom_call" | custom-call | flops 9865003008 | bytes 38535168 | tf_op jit(solution)/shard_map/pallas_call | solution.py:667
  133.4 3.0 %shard_map.47 = f32[128,12544]{1,0:T(8,128)} custom-call(f32[128,12544]{1,0:T(8,128)S(1)} %get-tuple-element.8.eig_ref, bf16[2,4,32,12544]{3,2,1,0:T(8,128)(2,1)S(1)} %get-tuple-element.9.wall_ref, bf16[128,256]{1,0:T(8,128)(2,1)S(1)} %get-tuple-element.10.coef_ref), custom_call_target="tpu_custom_call" | custom-call | flops 822083584 | bytes 12845056 | tf_op jit(solution)/shard_map/pallas_call | solution.py:727

commit v6 on v4

--- a/solution.py
+++ b/solution.py
@@ -107,7 +107,7 @@
     def cut(index):
         return pl.ds(pl.multiple_of(index * chunk, chunk), chunk)
 
-    short = max(1, chunk // LANES // 4) * LANES
+    short = max(1, chunk // LANES // 2) * LANES
     closing = (
         pl.ds(rows_dev - chunk, chunk - short),
         pl.ds(rows_dev - short, short),

time: 137 us -> 137 us (level)
  no operation moved by 1% of the time
where the time goes in v6:
time: 137 us
  Pallas kernels  137 us (100%)
    pallas_call x1, Pallas kernels, local(): pl.pallas_call(kernel, out_shape=(vmem(eigvecs.shape, F32), vmem((2, line...  133 us
    pallas_call x1, Pallas kernels, local(): pl.pallas_call(finish_kernel, out_shape=jax.ShapeDtypeStruct(eigvecs.shap...  3.1 us

profile of v6, /device:TPU:0, one launch (start us, length us, event | category | flops | bytes accessed | tf_op | source)
XLA Modules:
  0.0 136.7 jit_solution(10943985770209724540)
XLA Ops:
  0.0 133.5 %shard_map.46 = (f32[128,12544]{1,0:T(8,128)S(1)}, bf16[2,4,32,12544]{3,2,1,0:T(8,128)(2,1)S(1)}, bf16[128,256]{1,0:T(8,128)(2,1)S(1)}) custom-call(f32[128,12544]{1,0:T(8,128)} %eig_ref.1, f32[2,8,4,128]{3,2,1,0:T(4,128)} %vec_ref.1, s32[2,8]{1,0:T(2,128)} %off_ref.1, bf16[2,32,12544]{2,1,0:T(8,128)(2,1)} %pan_ref.1), custom_call_target="tpu_custom_call" | custom-call | flops 9865003008 | bytes 38535168 | tf_op jit(solution)/shard_map/pallas_call | solution.py:668
  133.5 3.1 %shard_map.47 = f32[128,12544]{1,0:T(8,128)} custom-call(f32[128,12544]{1,0:T(8,128)S(1)} %get-tuple-element.8.eig_ref, bf16[2,4,32,12544]{3,2,1,0:T(8,128)(2,1)S(1)} %get-tuple-element.9.wall_ref, bf16[128,256]{1,0:T(8,128)(2,1)S(1)} %get-tuple-element.10.coef_ref), custom_call_target="tpu_custom_call" | custom-call | flops 822083584 | bytes 12845056 | tf_op jit(solution)/shard_map/pallas_call | solution.py:728
